TPU v7x, 512 devices: a whole 4x8x8 slice. The times are simulated.
512 devices in a mesh: tile: 32 (over x, y), depth: 16 (over z, core).
Axes of the slice: x: 4, y: 8, z: 8, core: 2. Of those that a mesh axis runs over, the one named last changes fastest.
Arguments:
- samples: bfloat16 [16, 16, 16384, 128], P('depth', None, 'tile'), may hold values from -6 to 6
- opacity: float32 [16, 16, 16384], P('depth', None, 'tile'), may hold values from 0.004 to 0.06
- counts: int32 [16, 16384], P('depth', 'tile'), may hold values from 0 to 16
- depth_order: int32 [32, 16], P('tile'), may hold values from 0 to 15, each once within a row
- target: float32 [16384, 128], P(('tile', 'depth')), may hold values from -6 to 6
- weight_in: bfloat16 [16, 128, 256], P('depth'), may hold values from -0.5 to 0.5
- weight_out: bfloat16 [16, 256, 128], P('depth'), may hold values from -1.5 to 1.5
Outputs:
- pixels: float32 [16384, 128], P(('tile', 'depth'))
- grad_in: float32 [16, 128, 256], P('depth', 'tile')
- grad_out: float32 [16, 256, 128], P('depth', 'tile')
Inputs may be any that keep to these rules, and one draw needn't show every extreme that they name: `depth_order`: each row holds every brick rank 0 to 15 once.
All inputs are finite; a program needn't handle non-finite values.
Results may differ from a plain program's by a relative error of at most 0.0025.
Values sent between devices are 32-bit elements; how exact they have to be, the bound alone decides.
A program may use at most 64 MiB of HBM per device.

v0:
```python
import jax
import jax.numpy as jnp
from jax import lax
from jax.sharding import PartitionSpec as P


def in_order(tiles, dim):
    tiles = jnp.moveaxis(tiles, 0, dim)
    dims = tiles.shape
    return tiles.reshape(*dims[:dim], dims[dim] * dims[dim + 1], *dims[dim + 2 :])


def sent_to_all(array, axis):
    devices = lax.axis_size(axis)
    return lax.all_to_all(
        jnp.broadcast_to(array[None], (devices, *array.shape)), axis, 0, 0, tiled=True
    )


def gather_directly(array, axis, dim):
    return in_order(sent_to_all(array, axis), dim)


def cut_along(array, dim, devices):
    dims = array.shape
    tiles = array.reshape(*dims[:dim], devices, dims[dim] // devices, *dims[dim + 1 :])
    return jnp.moveaxis(tiles, dim, 0)


def sum_at_owner(array, axis, dim):
    tiles = cut_along(array, dim, lax.axis_size(axis))
    arrived = lax.all_to_all(tiles, axis, split_axis=0, concat_axis=0, tiled=True)
    return arrived.sum(axis=0)


def per_device(samples, opacity, counts, depth_order, target, weight_in, weight_out):
    inputs = samples[0]
    opaque = opacity[0]
    slot_total = opaque.shape[0]
    ray_total = opaque.shape[1]
    slot_index = lax.broadcasted_iota(jnp.int32, opaque.shape, 0)
    living = (slot_index < counts[0][None, :]).astype(jnp.float32)
    kept = 1.0 - opaque * living
    ones_row = jnp.ones((1, ray_total), jnp.float32)
    through = jnp.cumprod(jnp.concatenate([ones_row, kept[:-1]], axis=0), axis=0)
    contrib = living * opaque * through
    passing = jnp.prod(kept, axis=0)
    flat = inputs.reshape(slot_total * ray_total, inputs.shape[2])
    before_act = jnp.dot(flat, weight_in[0], preferred_element_type=jnp.float32)
    hidden = jnp.maximum(before_act, 0.0).astype(jnp.bfloat16)
    radiance = jnp.dot(hidden, weight_out[0], preferred_element_type=jnp.float32)
    radiance = radiance.reshape(slot_total, ray_total, radiance.shape[1])
    every_pass = gather_directly(passing[None, :], "depth", 0)
    brick_rank = depth_order[0]
    own_index = lax.axis_index("depth")
    picker = lax.broadcasted_iota(jnp.int32, brick_rank.shape, 0) == own_index
    own_rank = jnp.sum(jnp.where(picker, brick_rank, 0))
    in_front = brick_rank < own_rank
    veiling = jnp.prod(jnp.where(in_front[:, None], every_pass, 1.0), axis=0)
    factor = contrib * veiling[None, :]
    weighted = jnp.sum(factor[:, :, None] * radiance, axis=0)
    pixels = sum_at_owner(weighted, "depth", 0)
    pixel_grad = gather_directly(pixels - target, "depth", 0)
    feat_grad = (factor[:, :, None] * pixel_grad[None, :, :]).astype(jnp.bfloat16)
    feat_grad = feat_grad.reshape(slot_total * ray_total, feat_grad.shape[2])
    grad_out = jnp.dot(hidden.T, feat_grad, preferred_element_type=jnp.float32)
    hidden_grad = jnp.dot(feat_grad, weight_out[0].T, preferred_element_type=jnp.float32)
    hidden_grad = jnp.where(before_act > 0.0, hidden_grad, 0.0).astype(jnp.bfloat16)
    grad_in = jnp.dot(flat.T, hidden_grad, preferred_element_type=jnp.float32)
    grad_in, grad_out = (sum_at_owner(grad_in, "tile", 0), sum_at_owner(grad_out, "tile", 0))
    return (pixels, grad_in[None], grad_out[None])


def solution(mesh):
    placed = (
        P("depth", None, "tile", None),
        P("depth", None, "tile"),
        P("depth", "tile"),
        P("tile", None),
        P(("tile", "depth"), None),
        P("depth", None, None),
        P("depth", None, None),
    )
    return jax.shard_map(
        per_device,
        mesh=mesh,
        in_specs=placed,
        out_specs=(P(("tile", "depth"), None), P("depth", "tile", None), P("depth", "tile", None)),
        check_vma=False,
    )
```

profile of v0, /device:TPU:1, one launch (start us, length us, event | category | flops | bytes accessed | tf_op | source)
XLA Modules:
  0.0 102.5 jit_solution(12211154466958101047)
XLA Ops:
  0.6 0.0 copy-start
  0.6 0.9 fusion.14
  1.6 0.6 broadcast_in_dim.40
  2.2 11.8 %all-to-all-start = ((f32[16,1,512]{2,1,0:T(1,128)}), f32[16,1,512]{2,1,0:T(1,128)S(1)}, u32[]{:S(2)}, u32[]{:S(2)}) async-start(f32[16,1,512]{2,1,0:T(1,128)} %broadcast_in_dim.40), calls=%async_computation | async-start | bytes 65536 | tf_op jit(solution)/shard_map/all_to_all | solution.py:15
  14.0 1.3 %fusion.12 = s32[]{:T(128)} fusion(s32[1,16]{1,0:T(1,128)} %param.10, s32[]{:T(128)S(6)} %axis_index.12), kind=kLoop, calls=%fused_computation.20 | loop fusion | flops 47 | bytes 72 | tf_op jit(solution)/shard_map/reduce_sum | solution.py:57
  15.3 6.6 %maximum_convert_fusion = (bf16[8192,256]{1,0:T(8,128)(2,1)}, f32[8192,256]{1,0:T(8,128)}) fusion(bf16[8192,128]{1,0:T(8,128)(2,1)S(1)} %bitcast.48, bf16[1,128,256]{2,1,0:T(8,128)(2,1)} %param.12), kind=kOutput, calls=%fused_computation.2 | convolution fusion | flops 541065216 | bytes 14745600 | tf_op jit(solution)/shard_map/dot_general | solution.py:49
  21.9 0.7 bitcast_compare_fusion
  22.7 0.1 fusion.10
  22.8 3.1 %multiply_reduce_fusion = f32[512,128]{1,0:T(8,128)S(1)} fusion(bf16[16,512,256]{2,1,0:T(8,128)(2,1)} %bitcast.52, f32[16,512]{1,0:T(8,128)S(1)} %multiply_multiply_fusion, bf16[1,256,128]{2,1,0:T(8,128)(2,1)S(1)} %copy-done.2), kind=kOutput, calls=%fused_computation.6 | convolution fusion | flops 538902528 | bytes 4554752 | tf_op jit(solution)/shard_map/dot_general | solution.py:51
  25.9 18.6 %all_to_all.25 = f32[16,32,128]{2,1,0:T(8,128)S(1)} all-to-all(f32[16,32,128]{2,1,0:T(8,128)S(1)} %bitcast.55), channel_id=1, replica_groups=mesh['tile'=32,'depth'=16] {'depth'}, dimensions={0} | all-to-all | bytes 524288 | tf_op jit(solution)/shard_map/all_to_all | solution.py:32
  44.6 0.7 broadcast_in_dim.41
  45.3 3.4 %all-to-all-start.2 = ((f32[16,32,128]{2,1,0:T(8,128)}), f32[16,32,128]{2,1,0:T(8,128)S(1)}, u32[]{:S(2)}, u32[]{:S(2)}) async-start(f32[16,32,128]{2,1,0:T(8,128)} %broadcast_in_dim.41), calls=%async_computation.2 | async-start | bytes 524288 | tf_op jit(solution)/shard_map/all_to_all | solution.py:15
  48.8 6.4 %copy.13 = bf16[256,8192]{1,0:T(8,128)(2,1)} copy(bf16[256,8192]{0,1:T(8,128)(2,1)} %bitcast.53) | data formatting | bytes 8388608 | tf_op jit(solution)/shard_map/convert_element_type | solution.py:50
  55.1 4.8 %all-to-all-done.2 = f32[16,32,128]{2,1,0:T(8,128)S(1)} async-done(((f32[16,32,128]{2,1,0:T(8,128)}), f32[16,32,128]{2,1,0:T(8,128)S(1)}, u32[]{:S(2)}, u32[]{:S(2)}) %all-to-all-start.2) | async-done | bytes 262176 | tf_op jit(solution)/shard_map/all_to_all | solution.py:15
  59.9 2.2 %multiply_convert_fusion = bf16[16,512,128]{2,1,0:T(8,128)(2,1)} fusion(f32[512,128]{1,0:T(8,128)S(1)} %bitcast.54, f32[16,512]{1,0:T(8,128)S(1)} %multiply_multiply_fusion), kind=kLoop, calls=%fused_computation.5 | loop fusion | flops 2097152 | bytes 2392064 | tf_op jit(solution)/shard_map/convert_element_type | solution.py:64
  62.1 6.2 %fusion.4 = f32[128,256]{1,0:T(8,128)S(1)} fusion(bf16[8192,128]{1,0:T(8,128)(2,1)S(1)} %bitcast.49, bf16[8192,128]{1,0:T(8,128)(2,1)} %bitcast.50, f32[8192,256]{1,0:T(8,128)} %get-tuple-element.6, bf16[1,256,128]{2,1,0:T(8,128)(2,1)S(1)} %copy-done.2), kind=kOutput, calls=%fused_computation.8 | convolution fusion | flops 1080033280 | bytes 12779520 | tf_op jit(solution)/shard_map/dot_general | solution.py:69
  68.4 0.7 reshape.130
  69.0 9.7 %all-to-all-start.3 = ((f32[32,4,256]{2,1,0:T(4,128)}), f32[32,4,256]{2,1,0:T(4,128)S(1)}, u32[]{:S(2)}, u32[]{:S(2)}) async-start(f32[32,4,256]{2,1,0:T(4,128)} %reshape.130), calls=%async_computation.3 | async-start | bytes 262144 | tf_op jit(solution)/shard_map/all_to_all | solution.py:32
  78.7 4.8 %fusion.1 = f32[32,8,128]{2,1,0:T(8,128)} fusion(bf16[8192,128,1]{1,0,2:T(8,128)(2,1)} %bitcast.51, bf16[256,8192]{1,0:T(8,128)(2,1)} %copy.13), kind=kOutput, calls=%fused_computation.3 | convolution fusion | flops 536870912 | bytes 6422528 | tf_op jit(solution)/shard_map/dot_general | solution.py:66
  83.5 4.4 %all-to-all-done.3 = f32[32,4,256]{2,1,0:T(4,128)S(1)} async-done(((f32[32,4,256]{2,1,0:T(4,128)}), f32[32,4,256]{2,1,0:T(4,128)S(1)}, u32[]{:S(2)}, u32[]{:S(2)}) %all-to-all-start.3) | async-done | bytes 131104 | tf_op jit(solution)/shard_map/all_to_all | solution.py:32
  87.9 4.8 %all-to-all-start.4 = ((f32[32,8,128]{2,1,0:T(8,128)}), f32[32,8,128]{2,1,0:T(8,128)S(1)}, u32[]{:S(2)}, u32[]{:S(2)}) async-start(f32[32,8,128]{2,1,0:T(8,128)} %fusion.1), calls=%async_computation.4 | async-start | bytes 262144 | tf_op jit(solution)/shard_map/all_to_all | solution.py:32
  92.7 0.6 reduce_sum.48
  93.3 8.5 %all-to-all-done.4 = f32[32,8,128]{2,1,0:T(8,128)S(1)} async-done(((f32[32,8,128]{2,1,0:T(8,128)}), f32[32,8,128]{2,1,0:T(8,128)S(1)}, u32[]{:S(2)}, u32[]{:S(2)}) %all-to-all-start.4) | async-done | bytes 131104 | tf_op jit(solution)/shard_map/all_to_all | solution.py:32
  101.9 0.6 reduce_sum.49
  (18 shorter events, 0.1 us)
Async XLA Ops:
  0.6 14.7 %copy-start = (bf16[1,16,512,128]{3,2,1,0:T(8,128)(2,1)S(1)}, bf16[1,16,512,128]{3,2,1,0:T(8,128)(2,1)}, u32[]{:S(2)}) copy-start(bf16[1,16,512,128]{3,2,1,0:T(8,128)(2,1)} %param.7) | copy-start | bytes 6291460
  2.2 20.5 %all-to-all-start = ((f32[16,1,512]{2,1,0:T(1,128)}), f32[16,1,512]{2,1,0:T(1,128)S(1)}, u32[]{:S(2)}, u32[]{:S(2)}) async-start(f32[16,1,512]{2,1,0:T(1,128)} %broadcast_in_dim.40), calls=%async_computation | async-start | bytes 65536 | tf_op jit(solution)/shard_map/all_to_all | solution.py:15
  15.3 6.6 %copy-start.6 = (s32[1,16]{1,0:T(1,128)S(1)}, s32[1,16]{1,0:T(1,128)}, u32[]{:S(2)}) copy-start(s32[1,16]{1,0:T(1,128)} %param.10) | copy-start | bytes 196
  15.3 7.4 %copy-start.1 = (f32[1,16,512]{2,1,0:T(8,128)S(1)}, f32[1,16,512]{2,1,0:T(8,128)}, u32[]{:S(2)}) copy-start(f32[1,16,512]{2,1,0:T(8,128)} %param.8) | copy-start | bytes 98308
  15.3 7.4 %copy-start.5 = (s32[1,512]{1,0:T(1,128)S(1)}, s32[1,512]{1,0:T(1,128)}, u32[]{:S(2)}) copy-start(s32[1,512]{1,0:T(1,128)} %param.9) | copy-start | bytes 6148
  15.3 7.5 %copy-start.2 = (bf16[1,256,128]{2,1,0:T(8,128)(2,1)S(1)}, bf16[1,256,128]{2,1,0:T(8,128)(2,1)}, u32[]{:S(2)}) copy-start(bf16[1,256,128]{2,1,0:T(8,128)(2,1)} %param.13) | copy-start | bytes 196612
  21.9 22.6 %copy-start.4 = (f32[32,128]{1,0:T(8,128)S(1)}, f32[32,128]{1,0:T(8,128)}, u32[]{:S(2)}) copy-start(f32[32,128]{1,0:T(8,128)} %param.11) | copy-start | bytes 49156
  44.6 10.5 %copy-start.3 = (f32[32,128]{1,0:T(8,128)}, f32[32,128]{1,0:T(8,128)S(1)}, u32[]{:S(2)}) copy-start(f32[32,128]{1,0:T(8,128)S(1)} %reduce_sum.47) | copy-start | bytes 49156
  45.3 14.6 %all-to-all-start.2 = ((f32[16,32,128]{2,1,0:T(8,128)}), f32[16,32,128]{2,1,0:T(8,128)S(1)}, u32[]{:S(2)}, u32[]{:S(2)}) async-start(f32[16,32,128]{2,1,0:T(8,128)} %broadcast_in_dim.41), calls=%async_computation.2 | async-start | bytes 524288 | tf_op jit(solution)/shard_map/all_to_all | solution.py:15
  69.0 18.8 %all-to-all-start.3 = ((f32[32,4,256]{2,1,0:T(4,128)}), f32[32,4,256]{2,1,0:T(4,128)S(1)}, u32[]{:S(2)}, u32[]{:S(2)}) async-start(f32[32,4,256]{2,1,0:T(4,128)} %reshape.130), calls=%async_computation.3 | async-start | bytes 262144 | tf_op jit(solution)/shard_map/all_to_all | solution.py:32
  87.9 14.0 %all-to-all-start.4 = ((f32[32,8,128]{2,1,0:T(8,128)}), f32[32,8,128]{2,1,0:T(8,128)S(1)}, u32[]{:S(2)}, u32[]{:S(2)}) async-start(f32[32,8,128]{2,1,0:T(8,128)} %fusion.1), calls=%async_computation.4 | async-start | bytes 262144 | tf_op jit(solution)/shard_map/all_to_all | solution.py:32
where the time goes:
time: 104 us; the launch traced here: 102 us
  starting transfers between devices  29.8 us (29%)
  matrix products  20.7 us (20%)
  blocking collectives  18.6 us (18%)
  waiting for transfers between devices  17.7 us (17%)
  local copies, waits for them, and re-layouts  8.41 us (8%)
  other arithmetic  6.53 us (6%)
    all_to_all x1, blocking collectives, sum_at_owner(): lax.all_to_all(tiles, axis, split_axis=0, concat_axis=0, tiled=True)  18.6 us
    all_to_all x2, starting transfers between devices, sent_to_all(): lax.all_to_all(jnp.broadcast_to(array[None], (devices, *array.shape)), ax...  15.2 us
    all_to_all x2, starting transfers between devices, sum_at_owner(): lax.all_to_all(tiles, axis, split_axis=0, concat_axis=0, tiled=True)  14.5 us
    all_to_all x2, waiting for transfers between devices, sum_at_owner(): lax.all_to_all(tiles, axis, split_axis=0, concat_axis=0, tiled=True)  12.9 us
    dot_general x1, matrix products, per_device(): before_act = jnp.dot(flat, weight_in[0], preferred_element_type=jnp.float32)  6.6 us
    convert_element_type x1, local copies, waits for them, and re-layouts, per_device(): hidden = jnp.maximum(before_act, 0.0).astype(jnp.bfloat16)  6.35 us
    dot_general x1, matrix products, per_device(): grad_in = jnp.dot(flat.T, hidden_grad, preferred_element_type=jnp.float32)  6.24 us
    all_to_all x2, waiting for transfers between devices, sent_to_all(): lax.all_to_all(jnp.broadcast_to(array[None], (devices, *array.shape)), ax...  4.79 us
  transfers between devices with their start and end apart: 4, of which 3 were waited for; matrix products, arithmetic and copies ran while one was open for 20% of the time, Pallas kernels for 0%

commit v1 on v0

v1 whole, which is shorter than its diff:
```python
import jax
import jax.numpy as jnp
from jax import lax
from jax.experimental import pallas as pl
from jax.experimental.pallas import tpu as pltpu
from jax.sharding import PartitionSpec as P

ENC, HID, FEAT, SLOTS, RAYS = 128, 256, 128, 16, 512
BRICKS, OWN = 16, 32
ZS, XS, YS = 8, 4, 8
PAIR = 2 * OWN
ROWS = SLOTS * PAIR
MESH = pl.DeviceIdType.MESH
F32, BF16 = jnp.float32, jnp.bfloat16


def dot(a, b):
    return jnp.dot(a, b, preferred_element_type=F32)


def dot_t(a, b):
    return lax.dot_general(a, b, (((1,), (1,)), ((), ())), preferred_element_type=F32)


def split(a):
    high = a.astype(BF16)
    return high, (a - high.astype(F32)).astype(BF16)


def far_first(k):
    return lax.rem(4 + (1 - 2 * lax.rem(k, 2)) * lax.div(k + 1, 2) + 8, 8)


def kernel(
    samples_h, opacity_h, counts_h, order_h, target_h, first_h, second_h,
    pixels_o, grad_in_o, grad_out_o,
    xs, op, cnt, order, tgt, w1, w2,
    passed, ct, vt, hid, total, wsend, wrecv, pgs, fst, gin, gout,
    xin, xout, ysin, ysout, yin, yout,
    load_sem, p_send, p_recv, w_send, w_recv, g_send, g_recv, f_send, f_recv,
    x_send, x_recv, y_send, y_recv,
):
    tile = lax.axis_index("tile")
    own = lax.axis_index("depth")
    zi, core = lax.div(own, 2), lax.rem(own, 2)
    xi, yi = lax.div(tile, YS), lax.rem(tile, YS)
    partner = 2 * zi + 1 - core

    barrier = pltpu.get_barrier_semaphore()

    def greet(t, d):
        pl.semaphore_signal(
            barrier, inc=1, device_id={"tile": t, "depth": d}, device_id_type=MESH
        )

    @pl.loop(1, BRICKS)
    def _(j):
        greet(tile, lax.rem(own + j, BRICKS))

    @pl.loop(1, XS)
    def _(j):
        greet(lax.rem(xi + j, XS) * YS + yi, own)

    @pl.loop(1, YS)
    def _(j):
        greet(xi * YS + lax.rem(yi + j, YS), own)

    loads = [
        pltpu.make_async_copy(a, b, load_sem.at[i])
        for i, (a, b) in enumerate(
            [
                (opacity_h.at[0], op), (counts_h, cnt), (first_h.at[0], w1),
                (samples_h.at[0], xs), (second_h.at[0], w2), (order_h, order),
                (target_h, tgt),
            ]
        )
    ]
    for load in loads:
        load.start()

    def remote(src, dst, send, recv, t, d):
        return pltpu.make_async_remote_copy(
            src_ref=src, dst_ref=dst, send_sem=send, recv_sem=recv,
            device_id={"tile": t, "depth": d}, device_id_type=MESH,
        )

    loads[0].wait()
    loads[1].wait()
    slot = lax.broadcasted_iota(jnp.int32, (SLOTS, RAYS), 0)
    living = jnp.where(slot < cnt[...], 1.0, 0.0).astype(F32)
    alpha = op[...] * living
    kept = 1.0 - alpha
    through = jnp.ones((1, RAYS), F32)
    rows = []
    for s in range(SLOTS):
        rows.append(alpha[s : s + 1] * through)
        through = through * kept[s : s + 1]
    contrib = jnp.concatenate(rows + [jnp.zeros((128 - SLOTS, RAYS), F32)], axis=0)
    passed[own] = through
    ct[...] = contrib.T

    pl.semaphore_wait(barrier, BRICKS - 1 + XS - 1 + YS - 1)

    def p_copy(d):
        return remote(passed.at[own], passed.at[own], p_send.at[d], p_recv.at[own], tile, d)

    @pl.loop(0, BRICKS - 1)
    def _(j):
        p_copy(lax.rem(own + 8 + lax.div(j + 1, 2) * (1 - 2 * lax.rem(j, 2)) + BRICKS, BRICKS)).start()

    loads[2].wait()
    loads[3].wait()
    loads[4].wait()

    def w_copy(d):
        return remote(wsend.at[d], wrecv.at[own], w_send.at[d], w_recv.at[own], tile, d)

    def forward(zt):
        first_ray = pl.multiple_of(zt * PAIR, PAIR)
        rays = pl.ds(first_ray, PAIR)
        flat = xs[:, rays, :].reshape(ROWS, ENC)
        act = jnp.maximum(dot(flat, w1[...]), 0.0)
        hid[zt] = act.astype(BF16)
        cols = ct[rays, :]
        acc = jnp.zeros((PAIR, HID), F32)
        for s in range(SLOTS):
            acc = acc + act[s * PAIR : (s + 1) * PAIR] * cols[:, s : s + 1]
        total[rays, :] = acc
        high, low = split(acc)
        term = dot(high, w2[...]) + dot(low, w2[...])
        wsend[pl.ds(2 * zt, 2)] = term.reshape(2, OWN, FEAT)

    @pl.loop(0, ZS - 1)
    def _(k):
        zt = lax.rem(zi + far_first(k), ZS)
        forward(zt)
        w_copy(2 * zt).start()
        w_copy(2 * zt + 1).start()

    forward(zi)
    w_copy(partner).start()
    wrecv[own] = wsend[own]

    @pl.loop(0, ZS)
    def _(zt):
        rays = pl.ds(pl.multiple_of(zt * PAIR, PAIR), PAIR)
        cols = ct[rays, :]
        parts = []
        for s in range(SLOTS):
            parts.append((xs[s, rays, :].astype(F32) * cols[:, s : s + 1]).astype(BF16))
        fst[zt] = jnp.concatenate(parts, axis=0).T

    loads[5].wait()
    loads[6].wait()

    @pl.loop(1, BRICKS)
    def _(j):
        d = lax.rem(own + j, BRICKS)
        remote(passed.at[d], passed.at[d], p_send.at[d], p_recv.at[d], tile, d).wait_recv()

    every = jnp.concatenate([passed[b] for b in range(BRICKS)], axis=0)
    rank = order[...].astype(F32)
    grid = (BRICKS, BRICKS)
    ranks = jnp.broadcast_to(rank, grid)
    eye = lax.broadcasted_iota(jnp.int32, grid, 0) == lax.broadcasted_iota(jnp.int32, grid, 1)
    rank_col = jnp.sum(jnp.where(eye, ranks, 0.0), axis=1, keepdims=True)
    veils = []
    for b in range(BRICKS):
        chosen = jnp.where(rank_col < rank[:, b : b + 1], every, 1.0)
        chosen = chosen[:8] * chosen[8:]
        chosen = chosen[:4] * chosen[4:]
        chosen = chosen[:2] * chosen[2:]
        veils.append(chosen[:1] * chosen[1:])
    veil = jnp.concatenate(veils, axis=0)
    brick = lax.broadcasted_iota(jnp.int32, (BRICKS, RAYS), 0)
    veil_own = jnp.sum(jnp.where(brick == own, veil, 0.0), axis=0, keepdims=True)
    vt[...] = jnp.concatenate([veil, veil_own, jnp.zeros((127 - BRICKS, RAYS), F32)], axis=0).T

    @pl.loop(1, BRICKS)
    def _(j):
        d = lax.rem(own + j, BRICKS)
        remote(wsend.at[d], wrecv.at[d], w_send.at[d], w_recv.at[d], tile, d).wait_recv()

    mine = vt[pl.ds(pl.multiple_of(own * OWN, OWN), OWN), :]
    pixels = jnp.zeros((OWN, FEAT), F32)
    for b in range(BRICKS):
        pixels = pixels + wrecv[b] * mine[:, b : b + 1]
    pixels_o[...] = pixels
    pgs[own] = pixels - tgt[...]

    def g_copy(d):
        return remote(pgs.at[own], pgs.at[own], g_send.at[d], g_recv.at[own], tile, d)

    def f_copy(b):
        return remote(pgs.at[b], pgs.at[b], f_send.at[b], f_recv.at[b], tile, partner)

    @pl.loop(0, ZS - 1)
    def _(k):
        g_copy(2 * lax.rem(zi + far_first(k), ZS) + core).start()

    g_copy(partner).start()

    gin[...] = jnp.zeros((ENC, HID), F32)
    gout[...] = jnp.zeros((HID, FEAT), F32)

    def backward(zt):
        rays = pl.ds(pl.multiple_of(zt * PAIR, PAIR), PAIR)
        grad = pgs[pl.ds(2 * zt, 2)].reshape(PAIR, FEAT)
        veil_col = vt[rays, BRICKS : BRICKS + 1]
        high, low = split(grad * veil_col)
        spread = (dot_t(high, w2[...]) + dot_t(low, w2[...])).astype(BF16)
        summed = total[rays, :].astype(BF16)
        gout[...] += dot(summed.T, high)
        parts = []
        for s in range(SLOTS):
            live = hid[zt, s * PAIR : (s + 1) * PAIR, :] > 0
            parts.append(jnp.where(live, spread, jnp.zeros_like(spread)))
        gin[...] += dot(fst[zt], jnp.concatenate(parts, axis=0))

    def wait_g(b):
        remote(pgs.at[b], pgs.at[b], g_send.at[b], g_recv.at[b], tile, b).wait_recv()

    wait_g(partner)
    backward(zi)

    def near_first(k):
        return lax.rem(zi + far_first(6 - k), ZS)

    @pl.loop(0, ZS - 1)
    def _(k):
        zt = near_first(k)
        wait_g(2 * zt + core)
        f_copy(2 * zt + core).start()

    @pl.loop(0, ZS - 1)
    def _(k):
        zt = near_first(k)
        f_copy(2 * zt + 1 - core).wait_recv()
        backward(zt)

    def x_copies(xt):
        t = xt * YS + yi
        rin, rout = pl.ds(pl.multiple_of(32 * xt, 32), 32), pl.ds(pl.multiple_of(64 * xt, 64), 64)
        return (
            remote(gout.at[rout], xout.at[xi], x_send.at[xt, 0], x_recv.at[xi, 0], t, own),
            remote(gin.at[rin], xin.at[xi], x_send.at[xt, 1], x_recv.at[xi, 1], t, own),
        )

    def x_arrivals(xt):
        t = xt * YS + yi
        rin, rout = pl.ds(pl.multiple_of(32 * xt, 32), 32), pl.ds(pl.multiple_of(64 * xt, 64), 64)
        return (
            remote(gout.at[rout], xout.at[xt], x_send.at[xt, 0], x_recv.at[xt, 0], t, own),
            remote(gin.at[rin], xin.at[xt], x_send.at[xt, 1], x_recv.at[xt, 1], t, own),
        )

    for j in (2, 1, 3):
        for copy in x_copies(lax.rem(xi + j, XS)):
            copy.start()
    xout[xi] = gout[pl.ds(pl.multiple_of(64 * xi, 64), 64), :]
    xin[xi] = gin[pl.ds(pl.multiple_of(32 * xi, 32), 32), :]
    for j in (1, 3, 2):
        for copy in x_arrivals(lax.rem(xi + j, XS)):
            copy.wait_recv()
    sum_out = xout[0] + xout[1] + xout[2] + xout[3]
    sum_in = xin[0] + xin[1] + xin[2] + xin[3]
    ysout[...] = sum_out.reshape(YS, 8, FEAT)
    for j in range(YS):
        ysin[j] = sum_in[4 * j : 4 * j + 4]

    def y_copies(yt):
        t = xi * YS + yt
        return (
            remote(ysout.at[yt], yout.at[yi], y_send.at[yt, 0], y_recv.at[yi, 0], t, own),
            remote(ysin.at[yt], yin.at[yi], y_send.at[yt, 1], y_recv.at[yi, 1], t, own),
        )

    def y_arrivals(yt):
        t = xi * YS + yt
        return (
            remote(ysout.at[yt], yout.at[yt], y_send.at[yt, 0], y_recv.at[yt, 0], t, own),
            remote(ysin.at[yt], yin.at[yt], y_send.at[yt, 1], y_recv.at[yt, 1], t, own),
        )

    @pl.loop(0, YS - 1)
    def _(k):
        for copy in y_copies(lax.rem(yi + far_first(k), YS)):
            copy.start()

    yout[yi] = ysout[yi]
    yin[yi] = ysin[yi]

    @pl.loop(1, YS)
    def _(j):
        for copy in y_arrivals(lax.rem(yi + j, YS)):
            copy.wait_recv()

    acc_out, acc_in = yout[0], yin[0]
    for j in range(1, YS):
        acc_out = acc_out + yout[j]
        acc_in = acc_in + yin[j]
    grad_out_o[0] = acc_out
    grad_in_o[0] = acc_in

    @pl.loop(1, BRICKS)
    def _(j):
        d = lax.rem(own + j, BRICKS)
        p_copy(d).wait_send()
        w_copy(d).wait_send()

    g_copy(partner).wait_send()

    @pl.loop(1, ZS)
    def _(j):
        d = 2 * lax.rem(zi + j, ZS) + core
        g_copy(d).wait_send()
        f_copy(d).wait_send()

    @pl.loop(1, XS)
    def _(j):
        for copy in x_copies(lax.rem(xi + j, XS)):
            copy.wait_send()

    @pl.loop(1, YS)
    def _(j):
        for copy in y_copies(lax.rem(yi + j, YS)):
            copy.wait_send()


def per_device(samples, opacity, counts, depth_order, target, weight_in, weight_out):
    any_space = pl.BlockSpec(memory_space=pl.ANY)
    vmem = pl.BlockSpec(memory_space=pltpu.VMEM)
    dma = pltpu.SemaphoreType.DMA
    return pl.pallas_call(
        kernel,
        out_shape=(
            jax.ShapeDtypeStruct((OWN, FEAT), F32),
            jax.ShapeDtypeStruct((1, 4, HID), F32),
            jax.ShapeDtypeStruct((1, 8, FEAT), F32),
        ),
        in_specs=[any_space] * 7,
        out_specs=(vmem, vmem, vmem),
        scratch_shapes=[
            pltpu.VMEM((SLOTS, RAYS, ENC), BF16),
            pltpu.VMEM((SLOTS, RAYS), F32),
            pltpu.VMEM((1, RAYS), jnp.int32),
            pltpu.VMEM((1, BRICKS), jnp.int32),
            pltpu.VMEM((OWN, FEAT), F32),
            pltpu.VMEM((ENC, HID), BF16),
            pltpu.VMEM((HID, FEAT), BF16),
            pltpu.VMEM((BRICKS, 1, RAYS), F32),
            pltpu.VMEM((RAYS, 128), F32),
            pltpu.VMEM((RAYS, 128), F32),
            pltpu.VMEM((ZS, ROWS, HID), BF16),
            pltpu.VMEM((RAYS, HID), F32),
            pltpu.VMEM((BRICKS, OWN, FEAT), F32),
            pltpu.VMEM((BRICKS, OWN, FEAT), F32),
            pltpu.VMEM((BRICKS, OWN, FEAT), F32),
            pltpu.VMEM((ZS, ENC, ROWS), BF16),
            pltpu.VMEM((ENC, HID), F32),
            pltpu.VMEM((HID, FEAT), F32),
            pltpu.VMEM((XS, 32, HID), F32),
            pltpu.VMEM((XS, 64, FEAT), F32),
            pltpu.VMEM((YS, 4, HID), F32),
            pltpu.VMEM((YS, 8, FEAT), F32),
            pltpu.VMEM((YS, 4, HID), F32),
            pltpu.VMEM((YS, 8, FEAT), F32),
            dma((7,)),
            dma((BRICKS,)), dma((BRICKS,)),
            dma((BRICKS,)), dma((BRICKS,)),
            dma((BRICKS,)), dma((BRICKS,)),
            dma((BRICKS,)), dma((BRICKS,)),
            dma((XS, 2)), dma((XS, 2)),
            dma((YS, 2)), dma((YS, 2)),
        ],
        compiler_params=pltpu.CompilerParams(collective_id=0, has_side_effects=True),
        name="field_step",
    )(samples, opacity, counts, depth_order, target, weight_in, weight_out)


def solution(mesh):
    placed = (
        P("depth", None, "tile", None),
        P("depth", None, "tile"),
        P("depth", "tile"),
        P("tile", None),
        P(("tile", "depth"), None),
        P("depth", None, None),
        P("depth", None, None),
    )
    return jax.shard_map(
        per_device,
        mesh=mesh,
        in_specs=placed,
        out_specs=(P(("tile", "depth"), None), P("depth", "tile", None), P("depth", "tile", None)),
        check_vma=False,
    )
```

time: 104 us -> 51.3 us (0.49); the launches traced: 102 us -> 51 us
  Pallas kernels: 0 us -> 46.5 us
  starting transfers between devices: 29.8 us -> 0 us
  matrix products: 20.7 us -> 0 us
  blocking collectives: 18.6 us -> 0 us
  waiting for transfers between devices: 17.7 us -> 0 us
  other arithmetic: 6.53 us -> 0 us
  local copies, waits for them, and re-layouts: 8.41 us -> 3.86 us
    pallas_call x0 -> x1, Pallas kernels: none -> 46.5 us  [per_device(): pl.pallas_call(kernel, out_shape=(jax.ShapeDtypeStruct((OWN, FEAT), F32),...]
    all_to_all x4 -> x0, starting transfers between devices: 29.8 us -> none  [the longest x2 15.2 us: sent_to_all(): lax.all_to_all(jnp.broadcast_to(array[None], (devices, *array.shape)), ax...]
    dot_general x4 -> x0, matrix products: 20.7 us -> none  [the longest x1 6.6 us: per_device(): before_act = jnp.dot(flat, weight_in[0], preferred_element_type=jnp.float32)]
    all_to_all x1 -> x0, blocking collectives: 18.6 us -> none  [sum_at_owner(): lax.all_to_all(tiles, axis, split_axis=0, concat_axis=0, tiled=True)]
    all_to_all x4 -> x0, waiting for transfers between devices: 17.7 us -> none  [the longest x2 12.9 us: sum_at_owner(): lax.all_to_all(tiles, axis, split_axis=0, concat_axis=0, tiled=True)]
    convert_element_type x1 -> x0, local copies, waits for them, and re-layouts: 6.35 us -> none  [per_device(): hidden = jnp.maximum(before_act, 0.0).astype(jnp.bfloat16)]
    unnamed x14 -> x3, local copies, waits for them, and re-layouts: 0.04 us -> 3.86 us
    reduce_sum x4 -> x0, other arithmetic: 2.58 us -> none  [the longest x1 1.29 us: per_device(): own_rank = jnp.sum(jnp.where(picker, brick_rank, 0))]
  transfers between devices with their start and end apart: 4 -> 0, of which waited for: 3 -> 0; matrix products, arithmetic and copies ran while one was open for 20% -> 0% of each run, Pallas kernels for 0% -> 0%
where the time goes in v1:
time: 51.3 us; the launch traced here: 51 us
  Pallas kernels  46.5 us (91%)
  local copies, waits for them, and re-layouts  3.86 us (8%)
  between operations  0.64 us (1%)
    pallas_call x1, Pallas kernels, per_device(): pl.pallas_call(kernel, out_shape=(jax.ShapeDtypeStruct((OWN, FEAT), F32),...  46.5 us
    unnamed x3, local copies, waits for them, and re-layouts  3.86 us

profile of v1, /device:TPU:1, one launch (start us, length us, event | category | flops | bytes accessed | tf_op | source)
XLA Modules:
  0.0 51.0 jit_solution(16050216303944281822)
XLA Ops:
  0.6 46.5 %field_step.1 = (f32[32,128]{1,0:T(8,128)}, f32[1,4,256]{2,1,0:T(4,128)}, f32[1,8,128]{2,1,0:T(8,128)}) custom-call(bf16[1,16,512,128]{3,2,1,0:T(8,128)(2,1)} %samples_h.1, f32[1,16,512]{2,1,0:T(8,128)} %opacity_h.1, s32[1,512]{1,0:T(1,128)} %counts_h.1, s32[1,16]{1,0:T(1,128)} %order_h.1, f32[32,128]{1,0:T(8,128)} %target_h.1, ...), custom_call_target="tpu_custom_call" | custom-call | tf_op jit(solution)/shard_map/field_step/pallas_call | solution.py:334
  47.1 1.3 %copy.13 = f32[32,128]{1,0:T(8,128)} copy(f32[32,128]{1,0:T(8,128)} %get-tuple-element.6) | data formatting | bytes 32768
  48.5 1.3 %copy.14 = f32[1,4,256]{2,1,0:T(4,128)} copy(f32[1,4,256]{2,1,0:T(4,128)} %get-tuple-element.7) | data formatting | bytes 8192
  49.7 1.3 %copy.15 = f32[1,8,128]{2,1,0:T(8,128)} copy(f32[1,8,128]{2,1,0:T(8,128)} %get-tuple-element.8) | data formatting | bytes 8192

commit v2 on v1

--- a/solution.py
+++ b/solution.py
@@ -7,6 +7,7 @@
 
 ENC, HID, FEAT, SLOTS, RAYS = 128, 256, 128, 16, 512
 BRICKS, OWN = 16, 32
+EARLY = 4
 ZS, XS, YS = 8, 4, 8
 PAIR = 2 * OWN
 ROWS = SLOTS * PAIR
@@ -37,7 +38,7 @@
     xs, op, cnt, order, tgt, w1, w2,
     passed, ct, vt, hid, total, wsend, wrecv, pgs, fst, gin, gout,
     xin, xout, ysin, ysout, yin, yout,
-    load_sem, p_send, p_recv, w_send, w_recv, g_send, g_recv, f_send, f_recv,
+    load_sem, chunk_sem, p_send, p_recv, w_send, w_recv, g_send, g_recv, f_send, f_recv,
     x_send, x_recv, y_send, y_recv,
 ):
     tile = lax.axis_index("tile")
@@ -46,37 +47,43 @@
     xi, yi = lax.div(tile, YS), lax.rem(tile, YS)
     partner = 2 * zi + 1 - core
 
-    barrier = pltpu.get_barrier_semaphore()
-
-    def greet(t, d):
-        pl.semaphore_signal(
-            barrier, inc=1, device_id={"tile": t, "depth": d}, device_id_type=MESH
-        )
-
-    @pl.loop(1, BRICKS)
-    def _(j):
-        greet(tile, lax.rem(own + j, BRICKS))
-
-    @pl.loop(1, XS)
-    def _(j):
-        greet(lax.rem(xi + j, XS) * YS + yi, own)
-
-    @pl.loop(1, YS)
-    def _(j):
-        greet(xi * YS + lax.rem(yi + j, YS), own)
-
     loads = [
         pltpu.make_async_copy(a, b, load_sem.at[i])
         for i, (a, b) in enumerate(
             [
                 (opacity_h.at[0], op), (counts_h, cnt), (first_h.at[0], w1),
-                (samples_h.at[0], xs), (second_h.at[0], w2), (order_h, order),
-                (target_h, tgt),
+                (second_h.at[0], w2), (order_h, order), (target_h, tgt),
             ]
         )
     ]
-    for load in loads:
+    for load in loads[:3]:
         load.start()
+
+    def rays_of(zt):
+        return pl.ds(pl.multiple_of(zt * PAIR, PAIR), PAIR)
+
+    def fetch(k):
+        rays = rays_of(lax.rem(zi + far_first(k), ZS))
+        return pltpu.make_async_copy(samples_h.at[0, :, rays, :], xs.at[:, rays, :], chunk_sem.at[k])
+
+    for k in range(ZS):
+        fetch(k).start()
+    for load in loads[3:]:
+        load.start()
+
+    barrier = pltpu.get_barrier_semaphore()
+
+    def greet(t, d):
+        pl.semaphore_signal(
+            barrier, inc=1, device_id={"tile": t, "depth": d}, device_id_type=MESH
+        )
+
+    for j in range(1, BRICKS):
+        greet(tile, lax.rem(own + j, BRICKS))
+    for j in range(1, XS):
+        greet(lax.rem(xi + j, XS) * YS + yi, own)
+    for j in range(1, YS):
+        greet(xi * YS + lax.rem(yi + j, YS), own)
 
     def remote(src, dst, send, recv, t, d):
         return pltpu.make_async_remote_copy(
@@ -99,25 +106,17 @@
     passed[own] = through
     ct[...] = contrib.T
 
-    pl.semaphore_wait(barrier, BRICKS - 1 + XS - 1 + YS - 1)
-
     def p_copy(d):
         return remote(passed.at[own], passed.at[own], p_send.at[d], p_recv.at[own], tile, d)
 
-    @pl.loop(0, BRICKS - 1)
-    def _(j):
-        p_copy(lax.rem(own + 8 + lax.div(j + 1, 2) * (1 - 2 * lax.rem(j, 2)) + BRICKS, BRICKS)).start()
-
     loads[2].wait()
     loads[3].wait()
-    loads[4].wait()
 
     def w_copy(d):
         return remote(wsend.at[d], wrecv.at[own], w_send.at[d], w_recv.at[own], tile, d)
 
     def forward(zt):
-        first_ray = pl.multiple_of(zt * PAIR, PAIR)
-        rays = pl.ds(first_ray, PAIR)
+        rays = rays_of(zt)
         flat = xs[:, rays, :].reshape(ROWS, ENC)
         act = jnp.maximum(dot(flat, w1[...]), 0.0)
         hid[zt] = act.astype(BF16)
@@ -130,28 +129,48 @@
         term = dot(high, w2[...]) + dot(low, w2[...])
         wsend[pl.ds(2 * zt, 2)] = term.reshape(2, OWN, FEAT)
 
-    @pl.loop(0, ZS - 1)
-    def _(k):
-        zt = lax.rem(zi + far_first(k), ZS)
-        forward(zt)
+    def send_pair(zt):
         w_copy(2 * zt).start()
         w_copy(2 * zt + 1).start()
 
+    @pl.loop(0, EARLY)
+    def _(k):
+        fetch(k).wait()
+        forward(lax.rem(zi + far_first(k), ZS))
+
+    pl.semaphore_wait(barrier, BRICKS - 1 + XS - 1 + YS - 1)
+
+    @pl.loop(0, BRICKS - 1)
+    def _(j):
+        p_copy(lax.rem(own + 8 + lax.div(j + 1, 2) * (1 - 2 * lax.rem(j, 2)) + BRICKS, BRICKS)).start()
+
+    @pl.loop(0, EARLY)
+    def _(k):
+        send_pair(lax.rem(zi + far_first(k), ZS))
+
+    @pl.loop(EARLY, ZS - 1)
+    def _(k):
+        zt = lax.rem(zi + far_first(k), ZS)
+        fetch(k).wait()
+        forward(zt)
+        send_pair(zt)
+
+    fetch(ZS - 1).wait()
     forward(zi)
     w_copy(partner).start()
     wrecv[own] = wsend[own]
 
     @pl.loop(0, ZS)
     def _(zt):
-        rays = pl.ds(pl.multiple_of(zt * PAIR, PAIR), PAIR)
+        rays = rays_of(zt)
         cols = ct[rays, :]
         parts = []
         for s in range(SLOTS):
             parts.append((xs[s, rays, :].astype(F32) * cols[:, s : s + 1]).astype(BF16))
         fst[zt] = jnp.concatenate(parts, axis=0).T
 
+    loads[4].wait()
     loads[5].wait()
-    loads[6].wait()
 
     @pl.loop(1, BRICKS)
     def _(j):
@@ -204,7 +223,7 @@
     gout[...] = jnp.zeros((HID, FEAT), F32)
 
     def backward(zt):
-        rays = pl.ds(pl.multiple_of(zt * PAIR, PAIR), PAIR)
+        rays = rays_of(zt)
         grad = pgs[pl.ds(2 * zt, 2)].reshape(PAIR, FEAT)
         veil_col = vt[rays, BRICKS : BRICKS + 1]
         high, low = split(grad * veil_col)
@@ -220,23 +239,29 @@
     def wait_g(b):
         remote(pgs.at[b], pgs.at[b], g_send.at[b], g_recv.at[b], tile, b).wait_recv()
 
-    wait_g(partner)
-    backward(zi)
-
     def near_first(k):
         return lax.rem(zi + far_first(6 - k), ZS)
 
-    @pl.loop(0, ZS - 1)
-    def _(k):
-        zt = near_first(k)
-        wait_g(2 * zt + core)
-        f_copy(2 * zt + core).start()
-
-    @pl.loop(0, ZS - 1)
-    def _(k):
+    def relay(k):
+        b = 2 * near_first(k) + core
+        wait_g(b)
+        f_copy(b).start()
+
+    def settle(k):
         zt = near_first(k)
         f_copy(2 * zt + 1 - core).wait_recv()
         backward(zt)
+
+    wait_g(partner)
+    backward(zi)
+    relay(0)
+
+    @pl.loop(1, ZS - 1)
+    def _(k):
+        relay(k)
+        settle(k - 1)
+
+    settle(ZS - 2)
 
     def x_copies(xt):
         t = xt * YS + yi
@@ -327,18 +352,32 @@
             copy.wait_send()
 
 
+def write(pixels, grad_in, grad_out, pixels_o, grad_in_o, grad_out_o, sem):
+    copies = [
+        pltpu.make_async_copy(a, b, sem.at[i])
+        for i, (a, b) in enumerate(
+            [(pixels, pixels_o), (grad_in, grad_in_o), (grad_out, grad_out_o)]
+        )
+    ]
+    for copy in copies:
+        copy.start()
+    for copy in copies:
+        copy.wait()
+
+
 def per_device(samples, opacity, counts, depth_order, target, weight_in, weight_out):
-    any_space = pl.BlockSpec(memory_space=pl.ANY)
+    in_hbm = pl.BlockSpec(memory_space=pltpu.HBM)
     vmem = pl.BlockSpec(memory_space=pltpu.VMEM)
     dma = pltpu.SemaphoreType.DMA
-    return pl.pallas_call(
+    shapes = (
+        jax.ShapeDtypeStruct((OWN, FEAT), F32),
+        jax.ShapeDtypeStruct((1, 4, HID), F32),
+        jax.ShapeDtypeStruct((1, 8, FEAT), F32),
+    )
+    results = pl.pallas_call(
         kernel,
-        out_shape=(
-            jax.ShapeDtypeStruct((OWN, FEAT), F32),
-            jax.ShapeDtypeStruct((1, 4, HID), F32),
-            jax.ShapeDtypeStruct((1, 8, FEAT), F32),
-        ),
-        in_specs=[any_space] * 7,
+        out_shape=shapes,
+        in_specs=[in_hbm] * 7,
         out_specs=(vmem, vmem, vmem),
         scratch_shapes=[
             pltpu.VMEM((SLOTS, RAYS, ENC), BF16),
@@ -365,7 +404,7 @@
             pltpu.VMEM((YS, 8, FEAT), F32),
             pltpu.VMEM((YS, 4, HID), F32),
             pltpu.VMEM((YS, 8, FEAT), F32),
-            dma((7,)),
+            dma((6,)), dma((ZS,)),
             dma((BRICKS,)), dma((BRICKS,)),
             dma((BRICKS,)), dma((BRICKS,)),
             dma((BRICKS,)), dma((BRICKS,)),
@@ -373,9 +412,23 @@
             dma((XS, 2)), dma((XS, 2)),
             dma((YS, 2)), dma((YS, 2)),
         ],
-        compiler_params=pltpu.CompilerParams(collective_id=0, has_side_effects=True),
+        compiler_params=pltpu.CompilerParams(
+            collective_id=0, has_side_effects=True, vmem_limit_bytes=32 * 2**20
+        ),
         name="field_step",
-    )(samples, opacity, counts, depth_order, target, weight_in, weight_out)
+    )(*(
+        pltpu.with_memory_space_constraint(a, pltpu.HBM)
+        for a in (samples, opacity, counts, depth_order, target, weight_in, weight_out)
+    ))
+    return pl.pallas_call(
+        write,
+        out_shape=shapes,
+        in_specs=[vmem] * 3,
+        out_specs=(in_hbm,) * 3,
+        scratch_shapes=[dma((3,))],
+        compiler_params=pltpu.CompilerParams(vmem_limit_bytes=2**20),
+        name="write_results",
+    )(*results)
 
 
 def solution(mesh):

time: 51.3 us -> 47.3 us (0.922)
  local copies, waits for them, and re-layouts: 3.86 us -> 0 us
    unnamed x3 -> x0, local copies, waits for them, and re-layouts: 3.86 us -> none
    pallas_call x1 -> x2, Pallas kernels: 46.5 us -> 46.5 us  [the longest x1 45.9 us: per_device(): pl.pallas_call(kernel, out_shape=shapes, in_specs=[in_hbm] * 7, out_specs...]
where the time goes in v2:
time: 47.3 us; the launch traced here: 47.2 us
  Pallas kernels  46.5 us (98%)
  between operations  0.64 us (1%)
    pallas_call x1, Pallas kernels, per_device(): pl.pallas_call(kernel, out_shape=shapes, in_specs=[in_hbm] * 7, out_specs...  45.9 us

profile of v2, /device:TPU:1, one launch (start us, length us, event | category | flops | bytes accessed | tf_op | source)
XLA Modules:
  0.0 47.2 jit_solution(4395472111191774059)
XLA Ops:
  0.6 45.9 %field_step.1 = (f32[32,128]{1,0:T(8,128)S(1)}, f32[1,4,256]{2,1,0:T(4,128)S(1)}, f32[1,8,128]{2,1,0:T(8,128)S(1)}) custom-call(bf16[1,16,512,128]{3,2,1,0:T(8,128)(2,1)} %samples_h.1, f32[1,16,512]{2,1,0:T(8,128)} %opacity_h.1, s32[1,512]{1,0:T(1,128)} %counts_h.1, s32[1,16]{1,0:T(1,128)} %order_h.1, f32[32,128]{1,0:T(8,128)} %target_h.1, ...), custom_call_target="tpu_custom_call" | custom-call | tf_op jit(solution)/shard_map/field_step/pallas_call | solution.py:377
  46.5 0.6 %write_results.1 = (f32[32,128]{1,0:T(8,128)}, f32[1,4,256]{2,1,0:T(4,128)}, f32[1,8,128]{2,1,0:T(8,128)}) custom-call(f32[32,128]{1,0:T(8,128)S(1)} %get-tuple-element.6.pixels, f32[1,4,256]{2,1,0:T(4,128)S(1)} %get-tuple-element.7.grad_in, f32[1,8,128]{2,1,0:T(8,128)S(1)} %get-tuple-element.8.grad_out), custom_call_target="tpu_custom_call" | custom-call | tf_op jit(solution)/shard_map/write_results/pallas_call | solution.py:423

commit v3 on v2

--- a/solution.py
+++ b/solution.py
@@ -7,10 +7,11 @@
 
 ENC, HID, FEAT, SLOTS, RAYS = 128, 256, 128, 16, 512
 BRICKS, OWN = 16, 32
-EARLY = 4
+EARLY = 3
 ZS, XS, YS = 8, 4, 8
 PAIR = 2 * OWN
 ROWS = SLOTS * PAIR
+HALF = SLOTS * OWN
 MESH = pl.DeviceIdType.MESH
 F32, BF16 = jnp.float32, jnp.bfloat16
 
@@ -36,9 +37,9 @@
     samples_h, opacity_h, counts_h, order_h, target_h, first_h, second_h,
     pixels_o, grad_in_o, grad_out_o,
     xs, op, cnt, order, tgt, w1, w2,
-    passed, ct, vt, hid, total, wsend, wrecv, pgs, fst, gin, gout,
+    passed, near, ct, vt, vc, hid, total, sums, wsend, wrecv, pgs, fst, gin, gout,
     xin, xout, ysin, ysout, yin, yout,
-    load_sem, chunk_sem, p_send, p_recv, w_send, w_recv, g_send, g_recv, f_send, f_recv,
+    load_sem, chunk_sem, n_send, n_recv, p_send, p_recv, w_send, w_recv, g_send, g_recv, f_send, f_recv,
     x_send, x_recv, y_send, y_recv,
 ):
     tile = lax.axis_index("tile")
@@ -47,6 +48,20 @@
     xi, yi = lax.div(tile, YS), lax.rem(tile, YS)
     partner = 2 * zi + 1 - core
 
+    barrier = pltpu.get_barrier_semaphore()
+
+    def greet(t, d):
+        pl.semaphore_signal(
+            barrier, inc=1, device_id={"tile": t, "depth": d}, device_id_type=MESH
+        )
+
+    for j in (8, 9, 7, 10, 6, 11, 5, 12, 4, 13, 3, 14, 2, 15, 1):
+        greet(tile, lax.rem(own + j, BRICKS))
+    for j in range(1, XS):
+        greet(lax.rem(xi + j, XS) * YS + yi, own)
+    for j in range(1, YS):
+        greet(xi * YS + lax.rem(yi + j, YS), own)
+
     loads = [
         pltpu.make_async_copy(a, b, load_sem.at[i])
         for i, (a, b) in enumerate(
@@ -70,20 +85,6 @@
         fetch(k).start()
     for load in loads[3:]:
         load.start()
-
-    barrier = pltpu.get_barrier_semaphore()
-
-    def greet(t, d):
-        pl.semaphore_signal(
-            barrier, inc=1, device_id={"tile": t, "depth": d}, device_id_type=MESH
-        )
-
-    for j in range(1, BRICKS):
-        greet(tile, lax.rem(own + j, BRICKS))
-    for j in range(1, XS):
-        greet(lax.rem(xi + j, XS) * YS + yi, own)
-    for j in range(1, YS):
-        greet(xi * YS + lax.rem(yi + j, YS), own)
 
     def remote(src, dst, send, recv, t, d):
         return pltpu.make_async_remote_copy(
@@ -103,8 +104,14 @@
         rows.append(alpha[s : s + 1] * through)
         through = through * kept[s : s + 1]
     contrib = jnp.concatenate(rows + [jnp.zeros((128 - SLOTS, RAYS), F32)], axis=0)
-    passed[own] = through
+    for q in range(4):
+        passed[own, q] = through[:, 128 * q : 128 * q + 128]
     ct[...] = contrib.T
+
+    def n_copy(d):
+        return remote(
+            passed.at[own, lax.div(d, 4)], near.at[own], n_send.at[d], n_recv.at[own], tile, d
+        )
 
     def p_copy(d):
         return remote(passed.at[own], passed.at[own], p_send.at[d], p_recv.at[own], tile, d)
@@ -119,7 +126,9 @@
         rays = rays_of(zt)
         flat = xs[:, rays, :].reshape(ROWS, ENC)
         act = jnp.maximum(dot(flat, w1[...]), 0.0)
-        hid[zt] = act.astype(BF16)
+        rounded = act.astype(BF16).reshape(SLOTS, 2, OWN, HID)
+        for c in range(2):
+            hid[c, zt] = rounded[:, c].reshape(HALF, HID)
         cols = ct[rays, :]
         acc = jnp.zeros((PAIR, HID), F32)
         for s in range(SLOTS):
@@ -130,8 +139,9 @@
         wsend[pl.ds(2 * zt, 2)] = term.reshape(2, OWN, FEAT)
 
     def send_pair(zt):
-        w_copy(2 * zt).start()
-        w_copy(2 * zt + 1).start()
+        for d in (2 * zt, 2 * zt + 1):
+            n_copy(d).start()
+            w_copy(d).start()
 
     @pl.loop(0, EARLY)
     def _(k):
@@ -139,10 +149,6 @@
         forward(lax.rem(zi + far_first(k), ZS))
 
     pl.semaphore_wait(barrier, BRICKS - 1 + XS - 1 + YS - 1)
-
-    @pl.loop(0, BRICKS - 1)
-    def _(j):
-        p_copy(lax.rem(own + 8 + lax.div(j + 1, 2) * (1 - 2 * lax.rem(j, 2)) + BRICKS, BRICKS)).start()
 
     @pl.loop(0, EARLY)
     def _(k):
@@ -157,8 +163,18 @@
 
     fetch(ZS - 1).wait()
     forward(zi)
+    n_copy(partner).start()
     w_copy(partner).start()
     wrecv[own] = wsend[own]
+    near[own] = passed[own, lax.div(own, 4)]
+
+    @pl.loop(0, ZS - 1)
+    def _(k):
+        zt = lax.rem(zi + far_first(k), ZS)
+        p_copy(2 * zt).start()
+        p_copy(2 * zt + 1).start()
+
+    p_copy(partner).start()
 
     @pl.loop(0, ZS)
     def _(zt):
@@ -167,7 +183,9 @@
         parts = []
         for s in range(SLOTS):
             parts.append((xs[s, rays, :].astype(F32) * cols[:, s : s + 1]).astype(BF16))
-        fst[zt] = jnp.concatenate(parts, axis=0).T
+        for c in range(2):
+            half = jnp.concatenate([part[c * OWN : c * OWN + OWN] for part in parts], axis=0)
+            fst[c, zt] = half.T
 
     loads[4].wait()
     loads[5].wait()
@@ -175,32 +193,32 @@
     @pl.loop(1, BRICKS)
     def _(j):
         d = lax.rem(own + j, BRICKS)
-        remote(passed.at[d], passed.at[d], p_send.at[d], p_recv.at[d], tile, d).wait_recv()
-
-    every = jnp.concatenate([passed[b] for b in range(BRICKS)], axis=0)
+        remote(near.at[d], near.at[d], n_send.at[d], n_recv.at[d], tile, d).wait_recv()
+
     rank = order[...].astype(F32)
     grid = (BRICKS, BRICKS)
     ranks = jnp.broadcast_to(rank, grid)
-    eye = lax.broadcasted_iota(jnp.int32, grid, 0) == lax.broadcasted_iota(jnp.int32, grid, 1)
-    rank_col = jnp.sum(jnp.where(eye, ranks, 0.0), axis=1, keepdims=True)
-    veils = []
-    for b in range(BRICKS):
-        chosen = jnp.where(rank_col < rank[:, b : b + 1], every, 1.0)
+    row, col = (lax.broadcasted_iota(jnp.int32, grid, i) for i in range(2))
+    rank_col = jnp.sum(jnp.where(row == col, ranks, 0.0), axis=1, keepdims=True)
+    own_rank = jnp.sum(jnp.where(col[:1] == own, rank, 0.0), axis=1, keepdims=True)
+
+    def product(ahead, every):
+        chosen = jnp.where(rank_col < ahead, every, 1.0)
         chosen = chosen[:8] * chosen[8:]
         chosen = chosen[:4] * chosen[4:]
         chosen = chosen[:2] * chosen[2:]
-        veils.append(chosen[:1] * chosen[1:])
-    veil = jnp.concatenate(veils, axis=0)
-    brick = lax.broadcasted_iota(jnp.int32, (BRICKS, RAYS), 0)
-    veil_own = jnp.sum(jnp.where(brick == own, veil, 0.0), axis=0, keepdims=True)
-    vt[...] = jnp.concatenate([veil, veil_own, jnp.zeros((127 - BRICKS, RAYS), F32)], axis=0).T
+        return chosen[:1] * chosen[1:]
+
+    every = jnp.concatenate([near[b] for b in range(BRICKS)], axis=0)
+    veils = [product(rank[:, b : b + 1], every) for b in range(BRICKS)]
+    vt[...] = jnp.concatenate(veils + [jnp.zeros((128 - BRICKS, 128), F32)], axis=0).T
 
     @pl.loop(1, BRICKS)
     def _(j):
         d = lax.rem(own + j, BRICKS)
         remote(wsend.at[d], wrecv.at[d], w_send.at[d], w_recv.at[d], tile, d).wait_recv()
 
-    mine = vt[pl.ds(pl.multiple_of(own * OWN, OWN), OWN), :]
+    mine = vt[pl.ds(pl.multiple_of(lax.rem(own, 4) * OWN, OWN), OWN), :]
     pixels = jnp.zeros((OWN, FEAT), F32)
     for b in range(BRICKS):
         pixels = pixels + wrecv[b] * mine[:, b : b + 1]
@@ -219,57 +237,70 @@
 
     g_copy(partner).start()
 
-    gin[...] = jnp.zeros((ENC, HID), F32)
-    gout[...] = jnp.zeros((HID, FEAT), F32)
-
-    def backward(zt):
-        rays = rays_of(zt)
-        grad = pgs[pl.ds(2 * zt, 2)].reshape(PAIR, FEAT)
-        veil_col = vt[rays, BRICKS : BRICKS + 1]
-        high, low = split(grad * veil_col)
-        spread = (dot_t(high, w2[...]) + dot_t(low, w2[...])).astype(BF16)
-        summed = total[rays, :].astype(BF16)
-        gout[...] += dot(summed.T, high)
-        parts = []
-        for s in range(SLOTS):
-            live = hid[zt, s * PAIR : (s + 1) * PAIR, :] > 0
-            parts.append(jnp.where(live, spread, jnp.zeros_like(spread)))
-        gin[...] += dot(fst[zt], jnp.concatenate(parts, axis=0))
+    @pl.loop(1, BRICKS)
+    def _(j):
+        d = lax.rem(own + j, BRICKS)
+        remote(passed.at[d], passed.at[d], p_send.at[d], p_recv.at[d], tile, d).wait_recv()
+
+    for q in range(4):
+        every = jnp.concatenate([passed[b, q] for b in range(BRICKS)], axis=0)
+        veil = product(own_rank, every)
+        vc[128 * q : 128 * q + 128, :] = jnp.broadcast_to(veil, (128, 128)).T
+
+    for c in range(2):
+        half = jnp.concatenate(
+            [total[PAIR * z + OWN * c : PAIR * z + OWN * c + OWN, :] for z in range(ZS)], axis=0
+        )
+        sums[c] = half.T.astype(BF16)
+
+    @pl.loop(1, BRICKS)
+    def _(j):
+        d = lax.rem(own + j, BRICKS)
+        n_copy(d).wait_send()
+        p_copy(d).wait_send()
+        w_copy(d).wait_send()
 
     def wait_g(b):
         remote(pgs.at[b], pgs.at[b], g_send.at[b], g_recv.at[b], tile, b).wait_recv()
 
-    def near_first(k):
-        return lax.rem(zi + far_first(6 - k), ZS)
-
-    def relay(k):
-        b = 2 * near_first(k) + core
+    def gradient(c):
+        grads = jnp.concatenate([pgs[2 * z + c] for z in range(ZS)], axis=0)
+        cols = [vc[pl.ds(pl.multiple_of(PAIR * z + OWN * c, OWN), OWN), :] for z in range(ZS)]
+        high, low = split(grads * jnp.concatenate(cols, axis=0))
+        return high, (dot_t(high, w2[...]) + dot_t(low, w2[...])).astype(BF16)
+
+    def grad_in_of(c, spread):
+        acc = jnp.zeros((ENC, HID), F32)
+        for z in range(ZS):
+            mine = spread[OWN * z : OWN * z + OWN]
+            parts = []
+            for s in range(SLOTS):
+                live = hid[c, z, s * OWN : s * OWN + OWN, :] > 0
+                parts.append(jnp.where(live, mine, jnp.zeros_like(mine)))
+            acc = acc + dot(fst[c, z], jnp.concatenate(parts, axis=0))
+        return acc
+
+    for k in range(ZS - 1):
+        b = 2 * lax.rem(zi + far_first(6 - k), ZS) + core
         wait_g(b)
         f_copy(b).start()
 
-    def settle(k):
-        zt = near_first(k)
-        f_copy(2 * zt + 1 - core).wait_recv()
-        backward(zt)
+    high, spread = gradient(core)
+    gout[...] = dot(sums[core], high)
+    gin[...] = grad_in_of(core, spread)
 
     wait_g(partner)
-    backward(zi)
-    relay(0)
-
-    @pl.loop(1, ZS - 1)
-    def _(k):
-        relay(k)
-        settle(k - 1)
-
-    settle(ZS - 2)
-
-    def x_copies(xt):
+    for k in range(ZS - 1):
+        f_copy(2 * lax.rem(zi + far_first(6 - k), ZS) + 1 - core).wait_recv()
+
+    high, spread = gradient(1 - core)
+    gout[...] += dot(sums[1 - core], high)
+
+    def x_copies(xt, which=(0, 1)):
         t = xt * YS + yi
         rin, rout = pl.ds(pl.multiple_of(32 * xt, 32), 32), pl.ds(pl.multiple_of(64 * xt, 64), 64)
-        return (
-            remote(gout.at[rout], xout.at[xi], x_send.at[xt, 0], x_recv.at[xi, 0], t, own),
-            remote(gin.at[rin], xin.at[xi], x_send.at[xt, 1], x_recv.at[xi, 1], t, own),
-        )
+        ends = ((gout.at[rout], xout.at[xi]), (gin.at[rin], xin.at[xi]))
+        return [remote(*ends[i], x_send.at[xt, i], x_recv.at[xi, i], t, own) for i in which]
 
     def x_arrivals(xt):
         t = xt * YS + yi
@@ -280,10 +311,21 @@
         )
 
     for j in (2, 1, 3):
-        for copy in x_copies(lax.rem(xi + j, XS)):
-            copy.start()
+        x_copies(lax.rem(xi + j, XS), (0,))[0].start()
+    gin[...] += grad_in_of(1 - core, spread)
+    for j in (2, 1, 3):
+        x_copies(lax.rem(xi + j, XS), (1,))[0].start()
     xout[xi] = gout[pl.ds(pl.multiple_of(64 * xi, 64), 64), :]
     xin[xi] = gin[pl.ds(pl.multiple_of(32 * xi, 32), 32), :]
+
+    g_copy(partner).wait_send()
+
+    @pl.loop(1, ZS)
+    def _(j):
+        d = 2 * lax.rem(zi + j, ZS) + core
+        g_copy(d).wait_send()
+        f_copy(d).wait_send()
+
     for j in (1, 3, 2):
         for copy in x_arrivals(lax.rem(xi + j, XS)):
             copy.wait_recv()
@@ -307,16 +349,18 @@
             remote(ysin.at[yt], yin.at[yt], y_send.at[yt, 1], y_recv.at[yt, 1], t, own),
         )
 
-    @pl.loop(0, YS - 1)
-    def _(k):
-        for copy in y_copies(lax.rem(yi + far_first(k), YS)):
+    for j in (4, 3, 5, 2, 6, 1, 7):
+        for copy in y_copies(lax.rem(yi + j, YS)):
             copy.start()
 
     yout[yi] = ysout[yi]
     yin[yi] = ysin[yi]
 
-    @pl.loop(1, YS)
-    def _(j):
+    for j in range(1, XS):
+        for copy in x_copies(lax.rem(xi + j, XS)):
+            copy.wait_send()
+
+    for j in (1, 7, 2, 6, 3, 5, 4):
         for copy in y_arrivals(lax.rem(yi + j, YS)):
             copy.wait_recv()
 
@@ -327,27 +371,7 @@
     grad_out_o[0] = acc_out
     grad_in_o[0] = acc_in
 
-    @pl.loop(1, BRICKS)
-    def _(j):
-        d = lax.rem(own + j, BRICKS)
-        p_copy(d).wait_send()
-        w_copy(d).wait_send()
-
-    g_copy(partner).wait_send()
-
-    @pl.loop(1, ZS)
-    def _(j):
-        d = 2 * lax.rem(zi + j, ZS) + core
-        g_copy(d).wait_send()
-        f_copy(d).wait_send()
-
-    @pl.loop(1, XS)
-    def _(j):
-        for copy in x_copies(lax.rem(xi + j, XS)):
-            copy.wait_send()
-
-    @pl.loop(1, YS)
-    def _(j):
+    for j in range(1, YS):
         for copy in y_copies(lax.rem(yi + j, YS)):
             copy.wait_send()
 
@@ -387,15 +411,18 @@
             pltpu.VMEM((OWN, FEAT), F32),
             pltpu.VMEM((ENC, HID), BF16),
             pltpu.VMEM((HID, FEAT), BF16),
-            pltpu.VMEM((BRICKS, 1, RAYS), F32),
+            pltpu.VMEM((BRICKS, 4, 1, 128), F32),
+            pltpu.VMEM((BRICKS, 1, 128), F32),
             pltpu.VMEM((RAYS, 128), F32),
+            pltpu.VMEM((128, 128), F32),
             pltpu.VMEM((RAYS, 128), F32),
-            pltpu.VMEM((ZS, ROWS, HID), BF16),
+            pltpu.VMEM((2, ZS, HALF, HID), BF16),
             pltpu.VMEM((RAYS, HID), F32),
+            pltpu.VMEM((2, HID, RAYS // 2), BF16),
             pltpu.VMEM((BRICKS, OWN, FEAT), F32),
             pltpu.VMEM((BRICKS, OWN, FEAT), F32),
             pltpu.VMEM((BRICKS, OWN, FEAT), F32),
-            pltpu.VMEM((ZS, ENC, ROWS), BF16),
+            pltpu.VMEM((2, ZS, ENC, HALF), BF16),
             pltpu.VMEM((ENC, HID), F32),
             pltpu.VMEM((HID, FEAT), F32),
             pltpu.VMEM((XS, 32, HID), F32),
@@ -405,6 +432,7 @@
             pltpu.VMEM((YS, 4, HID), F32),
             pltpu.VMEM((YS, 8, FEAT), F32),
             dma((6,)), dma((ZS,)),
+            dma((BRICKS,)), dma((BRICKS,)),
             dma((BRICKS,)), dma((BRICKS,)),
             dma((BRICKS,)), dma((BRICKS,)),
             dma((BRICKS,)), dma((BRICKS,)),

time: 47.3 us -> 44.5 us (0.941)
  Pallas kernels: 46.5 us -> 43.7 us
    pallas_call x1, Pallas kernels: 45.9 us -> 43 us  [per_device(): pl.pallas_call(kernel, out_shape=shapes, in_specs=[in_hbm] * 7, out_specs...]
where the time goes in v3:
time: 44.5 us; the launch traced here: 44.3 us
  Pallas kernels  43.7 us (98%)
  between operations  0.64 us (1%)
    pallas_call x1, Pallas kernels, per_device(): pl.pallas_call(kernel, out_shape=shapes, in_specs=[in_hbm] * 7, out_specs...  43 us

profile of v3, /device:TPU:1, one launch (start us, length us, event | category | flops | bytes accessed | tf_op | source)
XLA Modules:
  0.0 44.3 jit_solution(1675433291696462390)
XLA Ops:
  0.6 43.0 %field_step.1 = (f32[32,128]{1,0:T(8,128)S(1)}, f32[1,4,256]{2,1,0:T(4,128)S(1)}, f32[1,8,128]{2,1,0:T(8,128)S(1)}) custom-call(bf16[1,16,512,128]{3,2,1,0:T(8,128)(2,1)} %samples_h.1, f32[1,16,512]{2,1,0:T(8,128)} %opacity_h.1, s32[1,512]{1,0:T(1,128)} %counts_h.1, s32[1,16]{1,0:T(1,128)} %order_h.1, f32[32,128]{1,0:T(8,128)} %target_h.1, ...), custom_call_target="tpu_custom_call" | custom-call | tf_op jit(solution)/shard_map/field_step/pallas_call | solution.py:401
  43.7 0.6 %write_results.1 = (f32[32,128]{1,0:T(8,128)}, f32[1,4,256]{2,1,0:T(4,128)}, f32[1,8,128]{2,1,0:T(8,128)}) custom-call(f32[32,128]{1,0:T(8,128)S(1)} %get-tuple-element.6.pixels, f32[1,4,256]{2,1,0:T(4,128)S(1)} %get-tuple-element.7.grad_in, f32[1,8,128]{2,1,0:T(8,128)S(1)} %get-tuple-element.8.grad_out), custom_call_target="tpu_custom_call" | custom-call | tf_op jit(solution)/shard_map/write_results/pallas_call | solution.py:451

commit v4 on v3

--- a/solution.py
+++ b/solution.py
@@ -108,19 +108,23 @@
         passed[own, q] = through[:, 128 * q : 128 * q + 128]
     ct[...] = contrib.T
 
+    def all_of(ref, count, sem):
+        part = ref.at[pl.ds(0, count)]
+        pltpu.make_async_copy(part, part, sem).wait()
+
     def n_copy(d):
         return remote(
-            passed.at[own, lax.div(d, 4)], near.at[own], n_send.at[d], n_recv.at[own], tile, d
+            passed.at[own, lax.div(d, 4)], near.at[own], n_send, n_recv, tile, d
         )
 
     def p_copy(d):
-        return remote(passed.at[own], passed.at[own], p_send.at[d], p_recv.at[own], tile, d)
+        return remote(passed.at[own], passed.at[own], p_send, p_recv, tile, d)
 
     loads[2].wait()
     loads[3].wait()
 
     def w_copy(d):
-        return remote(wsend.at[d], wrecv.at[own], w_send.at[d], w_recv.at[own], tile, d)
+        return remote(wsend.at[d], wrecv.at[own], w_send, w_recv, tile, d)
 
     def forward(zt):
         rays = rays_of(zt)
@@ -139,9 +143,8 @@
         wsend[pl.ds(2 * zt, 2)] = term.reshape(2, OWN, FEAT)
 
     def send_pair(zt):
-        for d in (2 * zt, 2 * zt + 1):
-            n_copy(d).start()
-            w_copy(d).start()
+        w_copy(2 * zt).start()
+        w_copy(2 * zt + 1).start()
 
     @pl.loop(0, EARLY)
     def _(k):
@@ -149,6 +152,9 @@
         forward(lax.rem(zi + far_first(k), ZS))
 
     pl.semaphore_wait(barrier, BRICKS - 1 + XS - 1 + YS - 1)
+
+    for j in (8, 9, 7, 10, 6, 11, 5, 12, 4, 13, 3, 14, 2, 15, 1):
+        n_copy(lax.rem(own + j, BRICKS)).start()
 
     @pl.loop(0, EARLY)
     def _(k):
@@ -163,7 +169,6 @@
 
     fetch(ZS - 1).wait()
     forward(zi)
-    n_copy(partner).start()
     w_copy(partner).start()
     wrecv[own] = wsend[own]
     near[own] = passed[own, lax.div(own, 4)]
@@ -190,10 +195,7 @@
     loads[4].wait()
     loads[5].wait()
 
-    @pl.loop(1, BRICKS)
-    def _(j):
-        d = lax.rem(own + j, BRICKS)
-        remote(near.at[d], near.at[d], n_send.at[d], n_recv.at[d], tile, d).wait_recv()
+    all_of(near, BRICKS - 1, n_recv)
 
     rank = order[...].astype(F32)
     grid = (BRICKS, BRICKS)
@@ -213,10 +215,7 @@
     veils = [product(rank[:, b : b + 1], every) for b in range(BRICKS)]
     vt[...] = jnp.concatenate(veils + [jnp.zeros((128 - BRICKS, 128), F32)], axis=0).T
 
-    @pl.loop(1, BRICKS)
-    def _(j):
-        d = lax.rem(own + j, BRICKS)
-        remote(wsend.at[d], wrecv.at[d], w_send.at[d], w_recv.at[d], tile, d).wait_recv()
+    all_of(wrecv, BRICKS - 1, w_recv)
 
     mine = vt[pl.ds(pl.multiple_of(lax.rem(own, 4) * OWN, OWN), OWN), :]
     pixels = jnp.zeros((OWN, FEAT), F32)
@@ -226,10 +225,10 @@
     pgs[own] = pixels - tgt[...]
 
     def g_copy(d):
-        return remote(pgs.at[own], pgs.at[own], g_send.at[d], g_recv.at[own], tile, d)
+        return remote(pgs.at[own], pgs.at[own], g_send, g_recv.at[zi], tile, d)
 
     def f_copy(b):
-        return remote(pgs.at[b], pgs.at[b], f_send.at[b], f_recv.at[b], tile, partner)
+        return remote(pgs.at[b], pgs.at[b], f_send, f_recv, tile, partner)
 
     @pl.loop(0, ZS - 1)
     def _(k):
@@ -237,10 +236,7 @@
 
     g_copy(partner).start()
 
-    @pl.loop(1, BRICKS)
-    def _(j):
-        d = lax.rem(own + j, BRICKS)
-        remote(passed.at[d], passed.at[d], p_send.at[d], p_recv.at[d], tile, d).wait_recv()
+    all_of(passed, BRICKS - 1, p_recv)
 
     for q in range(4):
         every = jnp.concatenate([passed[b, q] for b in range(BRICKS)], axis=0)
@@ -253,15 +249,12 @@
         )
         sums[c] = half.T.astype(BF16)
 
-    @pl.loop(1, BRICKS)
-    def _(j):
-        d = lax.rem(own + j, BRICKS)
-        n_copy(d).wait_send()
-        p_copy(d).wait_send()
-        w_copy(d).wait_send()
+    all_of(near, BRICKS - 1, n_send)
+    all_of(passed, BRICKS - 1, p_send)
+    all_of(wsend, BRICKS - 1, w_send)
 
     def wait_g(b):
-        remote(pgs.at[b], pgs.at[b], g_send.at[b], g_recv.at[b], tile, b).wait_recv()
+        pltpu.make_async_copy(pgs.at[b], pgs.at[b], g_recv.at[lax.div(b, 2)]).wait()
 
     def gradient(c):
         grads = jnp.concatenate([pgs[2 * z + c] for z in range(ZS)], axis=0)
@@ -290,45 +283,30 @@
     gin[...] = grad_in_of(core, spread)
 
     wait_g(partner)
-    for k in range(ZS - 1):
-        f_copy(2 * lax.rem(zi + far_first(6 - k), ZS) + 1 - core).wait_recv()
+    all_of(pgs, ZS - 1, f_recv)
 
     high, spread = gradient(1 - core)
     gout[...] += dot(sums[1 - core], high)
 
-    def x_copies(xt, which=(0, 1)):
+    def x_copies(xt, which):
         t = xt * YS + yi
         rin, rout = pl.ds(pl.multiple_of(32 * xt, 32), 32), pl.ds(pl.multiple_of(64 * xt, 64), 64)
-        ends = ((gout.at[rout], xout.at[xi]), (gin.at[rin], xin.at[xi]))
-        return [remote(*ends[i], x_send.at[xt, i], x_recv.at[xi, i], t, own) for i in which]
-
-    def x_arrivals(xt):
-        t = xt * YS + yi
-        rin, rout = pl.ds(pl.multiple_of(32 * xt, 32), 32), pl.ds(pl.multiple_of(64 * xt, 64), 64)
-        return (
-            remote(gout.at[rout], xout.at[xt], x_send.at[xt, 0], x_recv.at[xt, 0], t, own),
-            remote(gin.at[rin], xin.at[xt], x_send.at[xt, 1], x_recv.at[xt, 1], t, own),
-        )
+        src, dst = ((gout.at[rout], xout.at[xi]), (gin.at[rin], xin.at[xi]))[which]
+        return remote(src, dst, x_send.at[which], x_recv.at[which], t, own)
 
     for j in (2, 1, 3):
-        x_copies(lax.rem(xi + j, XS), (0,))[0].start()
+        x_copies(lax.rem(xi + j, XS), 0).start()
     gin[...] += grad_in_of(1 - core, spread)
     for j in (2, 1, 3):
-        x_copies(lax.rem(xi + j, XS), (1,))[0].start()
+        x_copies(lax.rem(xi + j, XS), 1).start()
     xout[xi] = gout[pl.ds(pl.multiple_of(64 * xi, 64), 64), :]
     xin[xi] = gin[pl.ds(pl.multiple_of(32 * xi, 32), 32), :]
 
-    g_copy(partner).wait_send()
-
-    @pl.loop(1, ZS)
-    def _(j):
-        d = 2 * lax.rem(zi + j, ZS) + core
-        g_copy(d).wait_send()
-        f_copy(d).wait_send()
-
-    for j in (1, 3, 2):
-        for copy in x_arrivals(lax.rem(xi + j, XS)):
-            copy.wait_recv()
+    all_of(pgs, ZS, g_send)
+    all_of(pgs, ZS - 1, f_send)
+
+    all_of(xout, XS - 1, x_recv.at[0])
+    all_of(xin, XS - 1, x_recv.at[1])
     sum_out = xout[0] + xout[1] + xout[2] + xout[3]
     sum_in = xin[0] + xin[1] + xin[2] + xin[3]
     ysout[...] = sum_out.reshape(YS, 8, FEAT)
@@ -338,15 +316,8 @@
     def y_copies(yt):
         t = xi * YS + yt
         return (
-            remote(ysout.at[yt], yout.at[yi], y_send.at[yt, 0], y_recv.at[yi, 0], t, own),
-            remote(ysin.at[yt], yin.at[yi], y_send.at[yt, 1], y_recv.at[yi, 1], t, own),
-        )
-
-    def y_arrivals(yt):
-        t = xi * YS + yt
-        return (
-            remote(ysout.at[yt], yout.at[yt], y_send.at[yt, 0], y_recv.at[yt, 0], t, own),
-            remote(ysin.at[yt], yin.at[yt], y_send.at[yt, 1], y_recv.at[yt, 1], t, own),
+            remote(ysout.at[yt], yout.at[yi], y_send.at[0], y_recv.at[0], t, own),
+            remote(ysin.at[yt], yin.at[yi], y_send.at[1], y_recv.at[1], t, own),
         )
 
     for j in (4, 3, 5, 2, 6, 1, 7):
@@ -356,13 +327,10 @@
     yout[yi] = ysout[yi]
     yin[yi] = ysin[yi]
 
-    for j in range(1, XS):
-        for copy in x_copies(lax.rem(xi + j, XS)):
-            copy.wait_send()
-
-    for j in (1, 7, 2, 6, 3, 5, 4):
-        for copy in y_arrivals(lax.rem(yi + j, YS)):
-            copy.wait_recv()
+    all_of(xout, XS - 1, x_send.at[0])
+    all_of(xin, XS - 1, x_send.at[1])
+    all_of(yout, YS - 1, y_recv.at[0])
+    all_of(yin, YS - 1, y_recv.at[1])
 
     acc_out, acc_in = yout[0], yin[0]
     for j in range(1, YS):
@@ -371,9 +339,8 @@
     grad_out_o[0] = acc_out
     grad_in_o[0] = acc_in
 
-    for j in range(1, YS):
-        for copy in y_copies(lax.rem(yi + j, YS)):
-            copy.wait_send()
+    all_of(yout, YS - 1, y_send.at[0])
+    all_of(yin, YS - 1, y_send.at[1])
 
 
 def write(pixels, grad_in, grad_out, pixels_o, grad_in_o, grad_out_o, sem):
@@ -432,13 +399,9 @@
             pltpu.VMEM((YS, 4, HID), F32),
             pltpu.VMEM((YS, 8, FEAT), F32),
             dma((6,)), dma((ZS,)),
-            dma((BRICKS,)), dma((BRICKS,)),
-            dma((BRICKS,)), dma((BRICKS,)),
-            dma((BRICKS,)), dma((BRICKS,)),
-            dma((BRICKS,)), dma((BRICKS,)),
-            dma((BRICKS,)), dma((BRICKS,)),
-            dma((XS, 2)), dma((XS, 2)),
-            dma((YS, 2)), dma((YS, 2)),
+            dma(()), dma(()), dma(()), dma(()), dma(()), dma(()),
+            dma(()), dma((ZS,)), dma(()), dma(()),
+            dma((2,)), dma((2,)), dma((2,)), dma((2,)),
         ],
         compiler_params=pltpu.CompilerParams(
             collective_id=0, has_side_effects=True, vmem_limit_bytes=32 * 2**20

time: 44.5 us -> 43 us (0.966)
  Pallas kernels: 43.7 us -> 42.2 us
    pallas_call x1, Pallas kernels: 43 us -> 41.6 us  [per_device(): pl.pallas_call(kernel, out_shape=shapes, in_specs=[in_hbm] * 7, out_specs...]
where the time goes in v4:
time: 43 us; the launch traced here: 42.9 us
  Pallas kernels  42.2 us (98%)
  between operations  0.64 us (1%)
    pallas_call x1, Pallas kernels, per_device(): pl.pallas_call(kernel, out_shape=shapes, in_specs=[in_hbm] * 7, out_specs...  41.6 us

profile of v4, /device:TPU:1, one launch (start us, length us, event | category | flops | bytes accessed | tf_op | source)
XLA Modules:
  0.0 42.9 jit_solution(15355215867659653549)
XLA Ops:
  0.6 41.6 %field_step.1 = (f32[32,128]{1,0:T(8,128)S(1)}, f32[1,4,256]{2,1,0:T(4,128)S(1)}, f32[1,8,128]{2,1,0:T(8,128)S(1)}) custom-call(bf16[1,16,512,128]{3,2,1,0:T(8,128)(2,1)} %samples_h.1, f32[1,16,512]{2,1,0:T(8,128)} %opacity_h.1, s32[1,512]{1,0:T(1,128)} %counts_h.1, s32[1,16]{1,0:T(1,128)} %order_h.1, f32[32,128]{1,0:T(8,128)} %target_h.1, ...), custom_call_target="tpu_custom_call" | custom-call | tf_op jit(solution)/shard_map/field_step/pallas_call | solution.py:368
  42.2 0.6 %write_results.1 = (f32[32,128]{1,0:T(8,128)}, f32[1,4,256]{2,1,0:T(4,128)}, f32[1,8,128]{2,1,0:T(8,128)}) custom-call(f32[32,128]{1,0:T(8,128)S(1)} %get-tuple-element.6.pixels, f32[1,4,256]{2,1,0:T(4,128)S(1)} %get-tuple-element.7.grad_in, f32[1,8,128]{2,1,0:T(8,128)S(1)} %get-tuple-element.8.grad_out), custom_call_target="tpu_custom_call" | custom-call | tf_op jit(solution)/shard_map/write_results/pallas_call | solution.py:414

commit v5 on v4

--- a/solution.py
+++ b/solution.py
@@ -9,6 +9,11 @@
 BRICKS, OWN = 16, 32
 EARLY = 3
 ZS, XS, YS = 8, 4, 8
+TILES = XS * YS
+FAR_TILES = sorted(
+    [(x, y) for x in range(XS) for y in range(YS) if x + y],
+    key=lambda d: -min(d[0], XS - d[0]) - min(d[1], YS - d[1]),
+)
 PAIR = 2 * OWN
 ROWS = SLOTS * PAIR
 HALF = SLOTS * OWN
@@ -38,9 +43,9 @@
     pixels_o, grad_in_o, grad_out_o,
     xs, op, cnt, order, tgt, w1, w2,
     passed, near, ct, vt, vc, hid, total, sums, wsend, wrecv, pgs, fst, gin, gout,
-    xin, xout, ysin, ysout, yin, yout,
+    grads, shares,
     load_sem, chunk_sem, n_send, n_recv, p_send, p_recv, w_send, w_recv, g_send, g_recv, f_send, f_recv,
-    x_send, x_recv, y_send, y_recv,
+    e_send, e_recv, met,
 ):
     tile = lax.axis_index("tile")
     own = lax.axis_index("depth")
@@ -173,6 +178,13 @@
     wrecv[own] = wsend[own]
     near[own] = passed[own, lax.div(own, 4)]
 
+    for j in range(1, XS):
+        pl.semaphore_signal(
+            met, inc=1,
+            device_id={"tile": lax.rem(xi + j, XS) * YS + yi, "depth": own},
+            device_id_type=MESH,
+        )
+
     @pl.loop(0, ZS - 1)
     def _(k):
         zt = lax.rem(zi + far_first(k), ZS)
@@ -286,61 +298,40 @@
     all_of(pgs, ZS - 1, f_recv)
 
     high, spread = gradient(1 - core)
-    gout[...] += dot(sums[1 - core], high)
-
-    def x_copies(xt, which):
-        t = xt * YS + yi
-        rin, rout = pl.ds(pl.multiple_of(32 * xt, 32), 32), pl.ds(pl.multiple_of(64 * xt, 64), 64)
-        src, dst = ((gout.at[rout], xout.at[xi]), (gin.at[rin], xin.at[xi]))[which]
-        return remote(src, dst, x_send.at[which], x_recv.at[which], t, own)
-
-    for j in (2, 1, 3):
-        x_copies(lax.rem(xi + j, XS), 0).start()
-    gin[...] += grad_in_of(1 - core, spread)
-    for j in (2, 1, 3):
-        x_copies(lax.rem(xi + j, XS), 1).start()
-    xout[xi] = gout[pl.ds(pl.multiple_of(64 * xi, 64), 64), :]
-    xin[xi] = gin[pl.ds(pl.multiple_of(32 * xi, 32), 32), :]
-
+    gout_total = gout[...] + dot(sums[1 - core], high)
+
+    def tile_at(dx, dy):
+        return lax.rem(xi + dx, XS) * YS + lax.rem(yi + dy, YS)
+
+    def e_copy(i, t):
+        return remote(grads.at[i, t], shares.at[i, tile], e_send.at[i], e_recv.at[i], t, own)
+
+    def scatter(i):
+        for dx, dy in FAR_TILES:
+            e_copy(i, tile_at(dx, dy)).start()
+
+    grads[0] = gout_total.reshape(TILES, 8, FEAT)
+    pl.semaphore_wait(met, XS - 1)
+    scatter(0)
+    total_in = gin[...] + grad_in_of(1 - core, spread)
+    for t in range(TILES):
+        rows = total_in[4 * t : 4 * t + 4]
+        grads[1, t] = jnp.concatenate([rows[:, :128], rows[:, 128:]], axis=0)
+    scatter(1)
+    for i in range(2):
+        shares[i, tile] = grads[i, tile]
     all_of(pgs, ZS, g_send)
     all_of(pgs, ZS - 1, f_send)
-
-    all_of(xout, XS - 1, x_recv.at[0])
-    all_of(xin, XS - 1, x_recv.at[1])
-    sum_out = xout[0] + xout[1] + xout[2] + xout[3]
-    sum_in = xin[0] + xin[1] + xin[2] + xin[3]
-    ysout[...] = sum_out.reshape(YS, 8, FEAT)
-    for j in range(YS):
-        ysin[j] = sum_in[4 * j : 4 * j + 4]
-
-    def y_copies(yt):
-        t = xi * YS + yt
-        return (
-            remote(ysout.at[yt], yout.at[yi], y_send.at[0], y_recv.at[0], t, own),
-            remote(ysin.at[yt], yin.at[yi], y_send.at[1], y_recv.at[1], t, own),
-        )
-
-    for j in (4, 3, 5, 2, 6, 1, 7):
-        for copy in y_copies(lax.rem(yi + j, YS)):
-            copy.start()
-
-    yout[yi] = ysout[yi]
-    yin[yi] = ysin[yi]
-
-    all_of(xout, XS - 1, x_send.at[0])
-    all_of(xin, XS - 1, x_send.at[1])
-    all_of(yout, YS - 1, y_recv.at[0])
-    all_of(yin, YS - 1, y_recv.at[1])
-
-    acc_out, acc_in = yout[0], yin[0]
-    for j in range(1, YS):
-        acc_out = acc_out + yout[j]
-        acc_in = acc_in + yin[j]
+    for i in range(2):
+        all_of(shares.at[i], TILES - 1, e_recv.at[i])
+    acc_out, acc_in = shares[0, 0], shares[1, 0]
+    for t in range(1, TILES):
+        acc_out = acc_out + shares[0, t]
+        acc_in = acc_in + shares[1, t]
     grad_out_o[0] = acc_out
-    grad_in_o[0] = acc_in
-
-    all_of(yout, YS - 1, y_send.at[0])
-    all_of(yin, YS - 1, y_send.at[1])
+    grad_in_o[0] = jnp.concatenate([acc_in[:4], acc_in[4:]], axis=1)
+    for i in range(2):
+        all_of(grads.at[i], TILES - 1, e_send.at[i])
 
 
 def write(pixels, grad_in, grad_out, pixels_o, grad_in_o, grad_out_o, sem):
@@ -392,16 +383,12 @@
             pltpu.VMEM((2, ZS, ENC, HALF), BF16),
             pltpu.VMEM((ENC, HID), F32),
             pltpu.VMEM((HID, FEAT), F32),
-            pltpu.VMEM((XS, 32, HID), F32),
-            pltpu.VMEM((XS, 64, FEAT), F32),
-            pltpu.VMEM((YS, 4, HID), F32),
-            pltpu.VMEM((YS, 8, FEAT), F32),
-            pltpu.VMEM((YS, 4, HID), F32),
-            pltpu.VMEM((YS, 8, FEAT), F32),
+            pltpu.VMEM((2, TILES, 8, 128), F32),
+            pltpu.VMEM((2, TILES, 8, 128), F32),
             dma((6,)), dma((ZS,)),
             dma(()), dma(()), dma(()), dma(()), dma(()), dma(()),
             dma(()), dma((ZS,)), dma(()), dma(()),
-            dma((2,)), dma((2,)), dma((2,)), dma((2,)),
+            dma((2,)), dma((2,)), pltpu.SemaphoreType.REGULAR,
         ],
         compiler_params=pltpu.CompilerParams(
             collective_id=0, has_side_effects=True, vmem_limit_bytes=32 * 2**20

time: 43 us -> 41.4 us (0.963)
  Pallas kernels: 42.2 us -> 40.6 us
    pallas_call x1, Pallas kernels: 41.6 us -> 39.9 us  [per_device(): pl.pallas_call(kernel, out_shape=shapes, in_specs=[in_hbm] * 7, out_specs...]
where the time goes in v5:
time: 41.4 us; the launch traced here: 41.2 us
  Pallas kernels  40.6 us (98%)
  between operations  0.64 us (2%)
    pallas_call x1, Pallas kernels, per_device(): pl.pallas_call(kernel, out_shape=shapes, in_specs=[in_hbm] * 7, out_specs...  39.9 us

profile of v5, /device:TPU:1, one launch (start us, length us, event | category | flops | bytes accessed | tf_op | source)
XLA Modules:
  0.0 41.2 jit_solution(7337546931326538273)
XLA Ops:
  0.6 39.9 %field_step.1 = (f32[32,128]{1,0:T(8,128)S(1)}, f32[1,4,256]{2,1,0:T(4,128)S(1)}, f32[1,8,128]{2,1,0:T(8,128)S(1)}) custom-call(bf16[1,16,512,128]{3,2,1,0:T(8,128)(2,1)} %samples_h.1, f32[1,16,512]{2,1,0:T(8,128)} %opacity_h.1, s32[1,512]{1,0:T(1,128)} %counts_h.1, s32[1,16]{1,0:T(1,128)} %order_h.1, f32[32,128]{1,0:T(8,128)} %target_h.1, ...), custom_call_target="tpu_custom_call" | custom-call | tf_op jit(solution)/shard_map/field_step/pallas_call | solution.py:359
  40.6 0.6 %write_results.1 = (f32[32,128]{1,0:T(8,128)}, f32[1,4,256]{2,1,0:T(4,128)}, f32[1,8,128]{2,1,0:T(8,128)}) custom-call(f32[32,128]{1,0:T(8,128)S(1)} %get-tuple-element.6.pixels, f32[1,4,256]{2,1,0:T(4,128)S(1)} %get-tuple-element.7.grad_in, f32[1,8,128]{2,1,0:T(8,128)S(1)} %get-tuple-element.8.grad_out), custom_call_target="tpu_custom_call" | custom-call | tf_op jit(solution)/shard_map/write_results/pallas_call | solution.py:401

commit v6 on v5

--- a/solution.py
+++ b/solution.py
@@ -7,7 +7,8 @@
 
 ENC, HID, FEAT, SLOTS, RAYS = 128, 256, 128, 16, 512
 BRICKS, OWN = 16, 32
-EARLY = 3
+EARLY = 2
+FAR = (4, 3, 5, 2, 6, 1, 7, 0)
 ZS, XS, YS = 8, 4, 8
 TILES = XS * YS
 FAR_TILES = sorted(
@@ -25,10 +26,6 @@
     return jnp.dot(a, b, preferred_element_type=F32)
 
 
-def dot_t(a, b):
-    return lax.dot_general(a, b, (((1,), (1,)), ((), ())), preferred_element_type=F32)
-
-
 def split(a):
     high = a.astype(BF16)
     return high, (a - high.astype(F32)).astype(BF16)
@@ -42,7 +39,7 @@
     samples_h, opacity_h, counts_h, order_h, target_h, first_h, second_h,
     pixels_o, grad_in_o, grad_out_o,
     xs, op, cnt, order, tgt, w1, w2,
-    passed, near, ct, vt, vc, hid, total, sums, wsend, wrecv, pgs, fst, gin, gout,
+    passed, near, ct, vt, vc, spread_veil, w2t, hid, total, sums, wsend, wrecv, pgs, fst, gin, gout,
     grads, shares,
     load_sem, chunk_sem, n_send, n_recv, p_send, p_recv, w_send, w_recv, g_send, g_recv, f_send, f_recv,
     e_send, e_recv, met,
@@ -83,7 +80,7 @@
         return pl.ds(pl.multiple_of(zt * PAIR, PAIR), PAIR)
 
     def fetch(k):
-        rays = rays_of(lax.rem(zi + far_first(k), ZS))
+        rays = rays_of(lax.rem(zi + FAR[k], ZS))
         return pltpu.make_async_copy(samples_h.at[0, :, rays, :], xs.at[:, rays, :], chunk_sem.at[k])
 
     for k in range(ZS):
@@ -131,49 +128,54 @@
     def w_copy(d):
         return remote(wsend.at[d], wrecv.at[own], w_send, w_recv, tile, d)
 
-    def forward(zt):
-        rays = rays_of(zt)
-        flat = xs[:, rays, :].reshape(ROWS, ENC)
-        act = jnp.maximum(dot(flat, w1[...]), 0.0)
-        rounded = act.astype(BF16).reshape(SLOTS, 2, OWN, HID)
-        for c in range(2):
-            hid[c, zt] = rounded[:, c].reshape(HALF, HID)
-        cols = ct[rays, :]
-        acc = jnp.zeros((PAIR, HID), F32)
-        for s in range(SLOTS):
-            acc = acc + act[s * PAIR : (s + 1) * PAIR] * cols[:, s : s + 1]
-        total[rays, :] = acc
-        high, low = split(acc)
-        term = dot(high, w2[...]) + dot(low, w2[...])
-        wsend[pl.ds(2 * zt, 2)] = term.reshape(2, OWN, FEAT)
+    def forward(targets):
+        acts = [
+            jnp.maximum(dot(xs[:, rays_of(zt), :].reshape(ROWS, ENC), w1[...]), 0.0)
+            for zt in targets
+        ]
+        accs = []
+        for zt, act in zip(targets, acts):
+            cols = ct[rays_of(zt), :]
+            acc = jnp.zeros((PAIR, HID), F32)
+            for s in range(SLOTS):
+                acc = acc + act[s * PAIR : (s + 1) * PAIR] * cols[:, s : s + 1]
+            accs.append(acc)
+        terms = []
+        for acc in accs:
+            high, low = split(acc)
+            terms.append(dot(high, w2[...]) + dot(low, w2[...]))
+        for zt, act, acc, term in zip(targets, acts, accs, terms):
+            wsend[pl.ds(2 * zt, 2)] = term.reshape(2, OWN, FEAT)
+            total[rays_of(zt), :] = acc
+            rounded = act.astype(BF16).reshape(SLOTS, 2, OWN, HID)
+            for c in range(2):
+                hid[c, zt] = rounded[:, c].reshape(HALF, HID)
 
     def send_pair(zt):
         w_copy(2 * zt).start()
         w_copy(2 * zt + 1).start()
 
-    @pl.loop(0, EARLY)
-    def _(k):
-        fetch(k).wait()
-        forward(lax.rem(zi + far_first(k), ZS))
+    targets = [lax.rem(zi + off, ZS) for off in FAR]
+
+    def compute(k):
+        fetch(2 * k).wait()
+        fetch(2 * k + 1).wait()
+        forward(targets[2 * k : 2 * k + 2])
+
+    for k in range(EARLY):
+        compute(k)
 
     pl.semaphore_wait(barrier, BRICKS - 1 + XS - 1 + YS - 1)
 
     for j in (8, 9, 7, 10, 6, 11, 5, 12, 4, 13, 3, 14, 2, 15, 1):
         n_copy(lax.rem(own + j, BRICKS)).start()
-
-    @pl.loop(0, EARLY)
-    def _(k):
-        send_pair(lax.rem(zi + far_first(k), ZS))
-
-    @pl.loop(EARLY, ZS - 1)
-    def _(k):
-        zt = lax.rem(zi + far_first(k), ZS)
-        fetch(k).wait()
-        forward(zt)
+    for zt in targets[: 2 * EARLY]:
         send_pair(zt)
-
-    fetch(ZS - 1).wait()
-    forward(zi)
+    for k in range(EARLY, 4):
+        compute(k)
+        for zt in targets[2 * k : 2 * k + 2][: 2 if k < 3 else 1]:
+            send_pair(zt)
+
     w_copy(partner).start()
     wrecv[own] = wsend[own]
     near[own] = passed[own, lax.div(own, 4)]
@@ -226,13 +228,17 @@
     every = jnp.concatenate([near[b] for b in range(BRICKS)], axis=0)
     veils = [product(rank[:, b : b + 1], every) for b in range(BRICKS)]
     vt[...] = jnp.concatenate(veils + [jnp.zeros((128 - BRICKS, 128), F32)], axis=0).T
+    mine = vt[pl.ds(pl.multiple_of(lax.rem(own, 4) * OWN, OWN), OWN), :]
+    for b in range(BRICKS):
+        spread_veil[b] = jnp.broadcast_to(mine[:, b : b + 1], (OWN, FEAT))
+    w2t[...] = w2[...].T
 
     all_of(wrecv, BRICKS - 1, w_recv)
 
-    mine = vt[pl.ds(pl.multiple_of(lax.rem(own, 4) * OWN, OWN), OWN), :]
-    pixels = jnp.zeros((OWN, FEAT), F32)
+    lanes = [jnp.zeros((OWN, FEAT), F32)] * 2
     for b in range(BRICKS):
-        pixels = pixels + wrecv[b] * mine[:, b : b + 1]
+        lanes[b % 2] = lanes[b % 2] + wrecv[b] * spread_veil[b]
+    pixels = lanes[0] + lanes[1]
     pixels_o[...] = pixels
     pgs[own] = pixels - tgt[...]
 
@@ -272,7 +278,7 @@
         grads = jnp.concatenate([pgs[2 * z + c] for z in range(ZS)], axis=0)
         cols = [vc[pl.ds(pl.multiple_of(PAIR * z + OWN * c, OWN), OWN), :] for z in range(ZS)]
         high, low = split(grads * jnp.concatenate(cols, axis=0))
-        return high, (dot_t(high, w2[...]) + dot_t(low, w2[...])).astype(BF16)
+        return high, (dot(high, w2t[...]) + dot(low, w2t[...])).astype(BF16)
 
     def grad_in_of(c, spread):
         acc = jnp.zeros((ENC, HID), F32)
@@ -374,6 +380,8 @@
             pltpu.VMEM((RAYS, 128), F32),
             pltpu.VMEM((128, 128), F32),
             pltpu.VMEM((RAYS, 128), F32),
+            pltpu.VMEM((BRICKS, OWN, FEAT), F32),
+            pltpu.VMEM((FEAT, HID), BF16),
             pltpu.VMEM((2, ZS, HALF, HID), BF16),
             pltpu.VMEM((RAYS, HID), F32),
             pltpu.VMEM((2, HID, RAYS // 2), BF16),

time: 41.4 us -> 41 us (level)
  no operation moved by 1% of the time
where the time goes in v6:
time: 41 us; the launch traced here: 40.9 us
  Pallas kernels  40.3 us (98%)
  between operations  0.64 us (2%)
    pallas_call x1, Pallas kernels, per_device(): pl.pallas_call(kernel, out_shape=shapes, in_specs=[in_hbm] * 7, out_specs...  39.6 us

profile of v6, /device:TPU:1, one launch (start us, length us, event | category | flops | bytes accessed | tf_op | source)
XLA Modules:
  0.0 40.9 jit_solution(15349258776403316280)
XLA Ops:
  0.6 39.6 %field_step.1 = (f32[32,128]{1,0:T(8,128)S(1)}, f32[1,4,256]{2,1,0:T(4,128)S(1)}, f32[1,8,128]{2,1,0:T(8,128)S(1)}) custom-call(bf16[1,16,512,128]{3,2,1,0:T(8,128)(2,1)} %samples_h.1, f32[1,16,512]{2,1,0:T(8,128)} %opacity_h.1, s32[1,512]{1,0:T(1,128)} %counts_h.1, s32[1,16]{1,0:T(1,128)} %order_h.1, f32[32,128]{1,0:T(8,128)} %target_h.1, ...), custom_call_target="tpu_custom_call" | custom-call | tf_op jit(solution)/shard_map/field_step/pallas_call | solution.py:365
  40.3 0.6 %write_results.1 = (f32[32,128]{1,0:T(8,128)}, f32[1,4,256]{2,1,0:T(4,128)}, f32[1,8,128]{2,1,0:T(8,128)}) custom-call(f32[32,128]{1,0:T(8,128)S(1)} %get-tuple-element.6.pixels, f32[1,4,256]{2,1,0:T(4,128)S(1)} %get-tuple-element.7.grad_in, f32[1,8,128]{2,1,0:T(8,128)S(1)} %get-tuple-element.8.grad_out), custom_call_target="tpu_custom_call" | custom-call | tf_op jit(solution)/shard_map/write_results/pallas_call | solution.py:409

commit v7 on v6

--- a/solution.py
+++ b/solution.py
@@ -81,7 +81,7 @@
 
     def fetch(k):
         rays = rays_of(lax.rem(zi + FAR[k], ZS))
-        return pltpu.make_async_copy(samples_h.at[0, :, rays, :], xs.at[:, rays, :], chunk_sem.at[k])
+        return pltpu.make_async_copy(samples_h.at[0, :, rays, :], xs.at[:, rays, :], chunk_sem.at[k // 2])
 
     for k in range(ZS):
         fetch(k).start()
@@ -158,8 +158,8 @@
     targets = [lax.rem(zi + off, ZS) for off in FAR]
 
     def compute(k):
-        fetch(2 * k).wait()
-        fetch(2 * k + 1).wait()
+        both = xs.at[:, pl.ds(0, 2 * PAIR), :]
+        pltpu.make_async_copy(both, both, chunk_sem.at[k]).wait()
         forward(targets[2 * k : 2 * k + 2])
 
     for k in range(EARLY):
@@ -281,15 +281,15 @@
         return high, (dot(high, w2t[...]) + dot(low, w2t[...])).astype(BF16)
 
     def grad_in_of(c, spread):
-        acc = jnp.zeros((ENC, HID), F32)
+        accs = [jnp.zeros((ENC, HID), F32)] * 2
         for z in range(ZS):
             mine = spread[OWN * z : OWN * z + OWN]
             parts = []
             for s in range(SLOTS):
                 live = hid[c, z, s * OWN : s * OWN + OWN, :] > 0
                 parts.append(jnp.where(live, mine, jnp.zeros_like(mine)))
-            acc = acc + dot(fst[c, z], jnp.concatenate(parts, axis=0))
-        return acc
+            accs[z % 2] = accs[z % 2] + dot(fst[c, z], jnp.concatenate(parts, axis=0))
+        return accs[0] + accs[1]
 
     for k in range(ZS - 1):
         b = 2 * lax.rem(zi + far_first(6 - k), ZS) + core
@@ -393,7 +393,7 @@
             pltpu.VMEM((HID, FEAT), F32),
             pltpu.VMEM((2, TILES, 8, 128), F32),
             pltpu.VMEM((2, TILES, 8, 128), F32),
-            dma((6,)), dma((ZS,)),
+            dma((6,)), dma((ZS // 2,)),
             dma(()), dma(()), dma(()), dma(()), dma(()), dma(()),
             dma(()), dma((ZS,)), dma(()), dma(()),
             dma((2,)), dma((2,)), pltpu.SemaphoreType.REGULAR,

time: 41 us -> 41.1 us (level)
  no operation moved by 1% of the time
where the time goes in v7:
time: 41.1 us; the launch traced here: 40.9 us
  Pallas kernels  40.3 us (98%)
  between operations  0.64 us (2%)
    pallas_call x1, Pallas kernels, per_device(): pl.pallas_call(kernel, out_shape=shapes, in_specs=[in_hbm] * 7, out_specs...  39.7 us

profile of v7, /device:TPU:1, one launch (start us, length us, event | category | flops | bytes accessed | tf_op | source)
XLA Modules:
  0.0 40.9 jit_solution(1246188363028632606)
XLA Ops:
  0.6 39.7 %field_step.1 = (f32[32,128]{1,0:T(8,128)S(1)}, f32[1,4,256]{2,1,0:T(4,128)S(1)}, f32[1,8,128]{2,1,0:T(8,128)S(1)}) custom-call(bf16[1,16,512,128]{3,2,1,0:T(8,128)(2,1)} %samples_h.1, f32[1,16,512]{2,1,0:T(8,128)} %opacity_h.1, s32[1,512]{1,0:T(1,128)} %counts_h.1, s32[1,16]{1,0:T(1,128)} %order_h.1, f32[32,128]{1,0:T(8,128)} %target_h.1, ...), custom_call_target="tpu_custom_call" | custom-call | tf_op jit(solution)/shard_map/field_step/pallas_call | solution.py:365
  40.3 0.6 %write_results.1 = (f32[32,128]{1,0:T(8,128)}, f32[1,4,256]{2,1,0:T(4,128)}, f32[1,8,128]{2,1,0:T(8,128)}) custom-call(f32[32,128]{1,0:T(8,128)S(1)} %get-tuple-element.6.pixels, f32[1,4,256]{2,1,0:T(4,128)S(1)} %get-tuple-element.7.grad_in, f32[1,8,128]{2,1,0:T(8,128)S(1)} %get-tuple-element.8.grad_out), custom_call_target="tpu_custom_call" | custom-call | tf_op jit(solution)/shard_map/write_results/pallas_call | solution.py:409
